TPU v7x, 32 devices: a whole 2x2x4 slice. The times are simulated.
32 devices in a mesh: aa: 8 (over z, y), ba: 4 (over x, core).
Axes of the slice: x: 2, y: 2, z: 4, core: 2. Of those that a mesh axis runs over, the one named last changes fastest.
Arguments:
- features: bfloat16 [65536, 256], P(('aa', 'ba')), may hold values from -6 to 6
- tile_ids: int32 [65536, 1], P(('aa', 'ba')), may hold values from 0 to 31; in each aligned block of 2048 rows (0 to 2047, 2048 to 4095, ...) at most 96 rows name the same one
- cell_ids: int32 [65536], P(('aa', 'ba')), may hold values from 0 to 8191
- spread_weight: float32 [65536], P(('aa', 'ba')), may hold values from 0.1 to 0.6
- read_weight: float32 [65536], P(('aa', 'ba')), may hold values from 0.5 to 2
- message_weight: bfloat16 [256, 256], replicated, may hold values from -0.375 to 0.375
- skip_weight: bfloat16 [256, 256], replicated, may hold values from -0.375 to 0.375
- spectral_weight: bfloat16 [16, 256, 256, 256], P('ba', 'aa'), may hold values from -1.5 to 1.5
- hidden_weight: bfloat16 [256, 256], replicated, may hold values from -0.375 to 0.375
- output_weight: bfloat16 [256, 256], replicated, may hold values from -0.75 to 0.75
Outputs:
- point_out: bfloat16 [65536, 256], P(('aa', 'ba'))
Inputs may be any that keep to these rules, and one draw needn't show every extreme that they name: `tile_ids`: among the rows of one device no index appears more than 96 times, and some index appears exactly 96 times.
All inputs are finite; a program needn't handle non-finite values.
Results may differ from a plain program's by a relative error of at most 0.015.
Values may be sent and summed in bfloat16 or wider, within the bound.
A program may use at most 64 MiB of HBM per device.

v0:
```python
import functools
import math

import jax
import jax.numpy as jnp
import numpy as np
from jax import lax
from jax.experimental import pallas as pl
from jax.experimental.pallas import tpu as pltpu
from jax.sharding import PartitionSpec as P

G = 64
F32 = jnp.float32
BF16 = jnp.bfloat16


def basis_np(modes, grid):
    k = np.arange(modes)[:, None]
    half = modes // 2
    freq = np.where(k < half, k, k - half + 1).astype(np.float64)
    phase = 2.0 * math.pi * freq * np.arange(grid)[None, :] / grid
    wave = np.where(k < half, np.cos(phase), np.sin(phase))
    norm = np.where(k == 0, math.sqrt(1.0 / grid), math.sqrt(2.0 / grid))
    return (wave * norm).astype(np.float32)


def split_table(table):
    high = table.astype(BF16)
    low = (table - high.astype(np.float32)).astype(BF16)
    return np.concatenate([high, low], axis=0)


def dot(a, b):
    return jnp.dot(a, b, preferred_element_type=F32)


def blocks_of(rows, want):
    return want if rows % want == 0 else rows


def pack_kernel(devices, capacity, tiles_ref, cells_ref, message_ref, rows_ref, where_ref, slots_ref, slots):
    block = rows_ref.shape[0]
    points = message_ref.shape[0]

    @pl.when(pl.program_id(0) == 0)
    def _():
        step = blocks_of(points, 256)
        upper = (
            lax.broadcasted_iota(jnp.int32, (step, step), 0)
            <= lax.broadcasted_iota(jnp.int32, (step, step), 1)
        ).astype(F32).astype(BF16)
        carry = jnp.zeros((devices, 1), F32)
        for start in range(0, points, step):
            tiles = tiles_ref[:, start : start + step]
            hot = (lax.broadcasted_iota(jnp.int32, (devices, step), 0) == tiles).astype(F32)
            counts = dot(hot.astype(BF16), upper) + carry
            rank = jnp.sum(counts * hot, axis=0, keepdims=True) - 1.0
            slots[:, start : start + step] = tiles * capacity + rank.astype(jnp.int32)
            carry = carry + jnp.sum(hot, axis=1, keepdims=True)
        slots_ref[...] = slots[...]

    own = lax.broadcasted_iota(jnp.int32, (block, points), 0) + pl.program_id(0) * block
    hot = (own == slots[...]).astype(F32).astype(BF16)
    rows_ref[...] = dot(hot, message_ref[...]).astype(BF16)
    found = dot(hot, cells_ref[...])
    where_ref[...] = found[:, 0:1] * G + found[:, 1:2] + (found[:, 2:3] - 1.0)


def pack(tiles, cells, message, devices, capacity):
    points, width = message.shape
    total = devices * capacity
    block = blocks_of(total, 256)
    return pl.pallas_call(
        functools.partial(pack_kernel, devices, capacity),
        grid=(total // block,),
        in_specs=[
            pl.BlockSpec((1, points), lambda i: (0, 0)),
            pl.BlockSpec(cells.shape, lambda i: (0, 0)),
            pl.BlockSpec((points, width), lambda i: (0, 0)),
        ],
        out_specs=[
            pl.BlockSpec((block, width), lambda i: (i, 0)),
            pl.BlockSpec((block, 1), lambda i: (i, 0)),
            pl.BlockSpec((1, points), lambda i: (0, 0)),
        ],
        out_shape=[
            jax.ShapeDtypeStruct((total, width), BF16),
            jax.ShapeDtypeStruct((total, 1), F32),
            jax.ShapeDtypeStruct((1, points), jnp.int32),
        ],
        scratch_shapes=[pltpu.VMEM((1, points), jnp.int32)],
        cost_estimate=pl.CostEstimate(
            flops=4 * total * points * width, bytes_accessed=6 * total * width, transcendentals=0
        ),
        name="pack",
    )(tiles, cells, message)


def merge_kernel(column_ref, row_ref, rows_ref, out_ref):
    same = (column_ref[...] == row_ref[...]).astype(F32).astype(BF16)
    out_ref[...] = dot(same, rows_ref[...]).astype(BF16)


def merge(where, rows):
    total, width = rows.shape
    block = blocks_of(total, 256)
    return pl.pallas_call(
        merge_kernel,
        grid=(total // block,),
        in_specs=[
            pl.BlockSpec((block, 1), lambda i: (i, 0)),
            pl.BlockSpec((1, total), lambda i: (0, 0)),
            pl.BlockSpec((total, width), lambda i: (0, 0)),
        ],
        out_specs=pl.BlockSpec((block, width), lambda i: (i, 0)),
        out_shape=jax.ShapeDtypeStruct((total, width), BF16),
        cost_estimate=pl.CostEstimate(
            flops=2 * total * total * width, bytes_accessed=4 * total * width, transcendentals=0
        ),
        name="merge",
    )(where.reshape(total, 1), where.reshape(1, total), rows)


def hot_rows(values, points):
    lane = lax.broadcasted_iota(jnp.int32, (2 * G, points), 0) % G
    return (lane == values).astype(F32).astype(BF16)


def hot_columns(values, points):
    lane = lax.broadcasted_iota(jnp.int32, (points, 2 * G), 1) % G
    return (lane == values).astype(F32).astype(BF16)


def forward_kernel(x_ref, y_ref, z_ref, tx_ref, ty_ref, tz_ref, message_ref, out_ref, plane, second):
    points = message_ref.shape[0]
    j = pl.program_id(0)

    @pl.when(j == 0)
    def _():
        plane[...] = dot(tx_ref[...], hot_rows(x_ref[...], points)) * dot(
            tz_ref[...], hot_rows(z_ref[...], points)
        )
        second[...] = dot(ty_ref[...], hot_rows(y_ref[...], points))

    scaled = (plane[...] * second[pl.ds(j, 1), :]).astype(BF16)
    result = dot(scaled, message_ref[...])
    out_ref[...] = result.reshape(out_ref.shape).astype(BF16)


def forward(x, y, z, tables, message, axis_first, modes):
    points, width = message.shape
    tx, ty, tz = tables
    pairs = tx.shape[1]
    share = pairs // axis_first
    whole = lambda shape: pl.BlockSpec(shape, lambda j: (0,) * len(shape))
    return pl.pallas_call(
        forward_kernel,
        grid=(modes,),
        in_specs=[whole((1, points))] * 3
        + [whole((pairs, 2 * G)), whole((modes, 2 * G)), whole((pairs, 2 * G)), whole((points, width))],
        out_specs=pl.BlockSpec((axis_first, 1, share, width), lambda j: (0, j, 0, 0)),
        out_shape=jax.ShapeDtypeStruct((axis_first, modes, share, width), BF16),
        scratch_shapes=[pltpu.VMEM((pairs, points), F32), pltpu.VMEM((modes, points), F32)],
        cost_estimate=pl.CostEstimate(
            flops=2 * modes * pairs * points * width,
            bytes_accessed=2 * modes * pairs * width,
            transcendentals=0,
        ),
        name="forward",
    )(x, y, z, tx.T, ty.T, tz.T, message)


def inverse_kernel(modes, x_ref, y_ref, z_ref, tx_ref, ty_ref, tz_ref, mixed_ref, out_ref):
    points, width = out_ref.shape
    pairs = tx_ref.shape[1]
    plane = dot(hot_columns(x_ref[...], points), tx_ref[...]) * dot(
        hot_columns(z_ref[...], points), tz_ref[...]
    )
    second = dot(hot_columns(y_ref[...], points), ty_ref[...])
    total = jnp.zeros((points, width), F32)
    for j in range(modes):
        part = mixed_ref[:, j]
        if part.shape[1] % 16:
            part = part.astype(F32)
        part = part.reshape(pairs, width).astype(BF16)
        total = total + dot((plane * second[:, j : j + 1]).astype(BF16), part)
    out_ref[...] = total


def inverse(x, y, z, tables, mixed):
    points = x.shape[0]
    tx, ty, tz = tables
    modes, width = mixed.shape[1], mixed.shape[3]
    pairs = tx.shape[1]
    block = blocks_of(points, 256)
    whole = lambda shape: pl.BlockSpec(shape, lambda i: (0,) * len(shape))
    column = pl.BlockSpec((block, 1), lambda i: (i, 0))
    return pl.pallas_call(
        functools.partial(inverse_kernel, modes),
        grid=(points // block,),
        in_specs=[column] * 3 + [whole(tx.shape), whole(ty.shape), whole(tz.shape), whole(mixed.shape)],
        out_specs=pl.BlockSpec((block, width), lambda i: (i, 0)),
        out_shape=jax.ShapeDtypeStruct((points, width), F32),
        cost_estimate=pl.CostEstimate(
            flops=2 * modes * pairs * points * width,
            bytes_accessed=2 * modes * pairs * width,
            transcendentals=0,
        ),
        name="inverse",
    )(x, y, z, tx, ty, tz, mixed)


def decode_kernel(slots_ref, returned_ref, inverse_ref, read_ref, skip_ref, hidden_ref, output_ref, out_ref):
    block = out_ref.shape[0]
    total = returned_ref.shape[0]
    lane = lax.broadcasted_iota(jnp.int32, (block, total), 1)
    hot = (lane == slots_ref[...]).astype(F32).astype(BF16)
    latent = dot(hot, returned_ref[...]).astype(BF16)
    latent_out = jax.nn.gelu(inverse_ref[...] + dot(latent, skip_ref[...])).astype(BF16)
    gathered = (read_ref[...] * latent_out.astype(F32)).astype(BF16)
    hidden = jax.nn.gelu(dot(gathered, hidden_ref[...])).astype(BF16)
    out_ref[...] = dot(hidden, output_ref[...]).astype(BF16)


def decode(slots, returned, inverse_values, read, skip_weight, hidden_weight, output_weight):
    points, width = inverse_values.shape
    total = returned.shape[0]
    block = blocks_of(points, 256)
    whole = lambda shape: pl.BlockSpec(shape, lambda i: (0,) * len(shape))
    column = pl.BlockSpec((block, 1), lambda i: (i, 0))
    rows = pl.BlockSpec((block, width), lambda i: (i, 0))
    return pl.pallas_call(
        decode_kernel,
        grid=(points // block,),
        in_specs=[column, whole((total, width)), rows, column] + [whole((width, width))] * 3,
        out_specs=rows,
        out_shape=jax.ShapeDtypeStruct((points, width), BF16),
        cost_estimate=pl.CostEstimate(
            flops=2 * points * total * width, bytes_accessed=4 * total * width, transcendentals=0
        ),
        name="decode",
    )(slots, returned, inverse_values, read, skip_weight, hidden_weight, output_weight)


def per_device(
    features,
    tile_ids,
    cell_ids,
    spread_weight,
    read_weight,
    message_weight,
    skip_weight,
    spectral_weight,
    hidden_weight,
    output_weight,
):
    axes = ("aa", "ba")
    points, width = features.shape
    axis_first = lax.axis_size("aa")
    axis_second = lax.axis_size("ba")
    devices = axis_first * axis_second
    capacity = 3 * points // (2 * devices)
    tile_x = G // axis_first
    tile_y = G // axis_second
    modes_y, share = spectral_weight.shape[0], spectral_weight.shape[1]
    modes = modes_y * axis_second

    basis = basis_np(modes, G)
    tx = split_table(np.repeat(basis, modes, axis=0).T)
    tz = split_table(np.tile(basis, (modes, 1)).T)
    ty = split_table(basis.T)
    tables = (jnp.asarray(tx), jnp.asarray(ty), jnp.asarray(tz))

    targets = tile_ids[:, 0]
    x = targets // axis_second * tile_x + cell_ids // (tile_y * G)
    y = targets % axis_second * tile_y + cell_ids // G % tile_y
    z = cell_ids % G

    product = dot(features, message_weight)
    message = (spread_weight[:, None] * product).astype(BF16)
    marks = jnp.stack([cell_ids // G, cell_ids % G, jnp.ones_like(cell_ids)], axis=1)
    marks = jnp.pad(marks.astype(BF16), ((0, 0), (0, 125)))
    send_rows, send_where, slots = pack(targets[None, :], marks, message, devices, capacity)
    recv_where = lax.all_to_all(
        send_where.reshape(devices, capacity), axes, split_axis=0, concat_axis=0, tiled=True
    )
    recv_rows = lax.all_to_all(send_rows, axes, split_axis=0, concat_axis=0, tiled=True)

    partial = forward(x[None, :], y[None, :], z[None, :], tables, message, axis_first, modes)
    partial = partial.reshape(devices, modes_y, share, width)
    partial = partial.reshape(axis_first, axis_second, modes_y, share, width)
    partial = lax.all_to_all(partial, 'ba', split_axis=1, concat_axis=1, tiled=True)
    partial = jnp.sum(partial.astype(F32), axis=1).astype(BF16)
    partial = lax.all_to_all(partial, 'aa', split_axis=0, concat_axis=0, tiled=True)
    spectrum = jnp.sum(partial.astype(F32), axis=0).astype(BF16)
    mixed = jnp.einsum(
        "jmc,jmco->jmo", spectrum, spectral_weight, preferred_element_type=F32
    ).astype(BF16)
    gathered = lax.all_gather(mixed, 'ba', axis=0, tiled=True)
    gathered = lax.all_gather(gathered, 'aa', axis=0)

    merged = merge(recv_where, recv_rows)
    returned = lax.all_to_all(merged, axes, split_axis=0, concat_axis=0, tiled=True)
    values = inverse(x[:, None], y[:, None], z[:, None], tables, gathered)
    return decode(
        slots.reshape(points, 1), returned, values, read_weight[:, None],
        skip_weight, hidden_weight, output_weight,
    )


def solution(mesh):
    placed = (
        P(("aa", "ba"), None),
        P(("aa", "ba"), None),
        P(("aa", "ba")),
        P(("aa", "ba")),
        P(("aa", "ba")),
        P(),
        P(),
        P("ba", "aa", None, None),
        P(),
        P(),
    )
    return jax.shard_map(
        per_device, mesh=mesh, in_specs=placed, out_specs=P(("aa", "ba"), None), check_vma=False
    )
```

profile of v0, /device:TPU:0, one launch (start us, length us, event | category | flops | bytes accessed | tf_op | source)
XLA Modules:
  0.0 212.2 jit_solution(13492753506645783550)
XLA Ops:
  6.5 0.0 copy-start
  6.5 1.4 fusion.7
  8.0 0.0 copy-done
  8.0 2.3 %fusion.message_ref = bf16[2048,256]{1,0:T(8,128)(2,1)} fusion(bf16[2048,256]{1,0:T(8,128)(2,1)S(1)} %copy-done, bf16[256,256]{1,0:T(8,128)(2,1)} %param.18, f32[2048]{0:T(1024)} %param.16), kind=kOutput, calls=%fused_computation.1 | convolution fusion | flops 269484032 | bytes 2236416 | tf_op jit(solution)/shard_map/dot_general | solution.py:34
  10.3 11.5 %forward.1 = bf16[8,16,32,256]{3,2,1,0:T(8,128)(2,1)} custom-call(s32[1,2048]{1,0:T(1,128)} %bitcast.39, s32[1,2048]{1,0:T(1,128)} %bitcast.37, s32[1,2048]{1,0:T(1,128)} %bitcast.34, bf16[256,128]{1,0:T(8,128)(2,1)} %constant.98.tx_ref, bf16[16,128]{1,0:T(8,128)(2,1)} %constant.99.ty_ref, bf16[256,128]{1,0:T(8,128)(2,1)} %constant.100.tz_ref, ...), custom_call_target="tpu_custom_call" | custom-call | flops 4294967296 | bytes 2097152 | tf_op jit(solution)/shard_map/forward/pallas_call | solution.py:156
  21.8 3.2 %copy.34 = bf16[8,4,4,32,256]{4,3,2,0,1:T(8,128)(2,1)} copy(bf16[8,4,4,32,256]{4,3,2,1,0:T(8,128)(2,1)} %bitcast.26) | data formatting | bytes 4194304 | tf_op jit(solution)/shard_map/reshape;reshape | solution.py:291
  25.0 0.0 copy-start.3
  25.0 4.4 %all-to-all-start.3 = ((bf16[8,4,4,32,256]{4,3,2,0,1:T(8,128)(2,1)}), bf16[8,4,4,32,256]{4,3,2,0,1:T(8,128)(2,1)S(1)}, u32[]{:S(2)}, u32[]{:S(2)}) async-start(bf16[8,4,4,32,256]{4,3,2,0,1:T(8,128)(2,1)} %copy.34), calls=%async_computation.3 | async-start | bytes 4194304 | tf_op jit(solution)/shard_map/all_to_all | solution.py:292
  29.4 0.0 copy-done.3
  29.4 0.1 pad.7.clone
  29.5 0.1 maximum_maximum_fusion
  29.5 1.1 copy.31
  30.6 2.0 pad.4.cells_ref
  32.6 11.8 %pack.1 = (bf16[3072,256]{1,0:T(8,128)(2,1)}, f32[3072,1]{1,0:T(8,128)}, s32[1,2048]{1,0:T(1,128)}) custom-call(s32[1,2048]{1,0:T(1,128)} %bitcast.44, bf16[2048,128]{1,0:T(8,128)(2,1)} %pad.4.cells_ref, bf16[2048,256]{1,0:T(8,128)(2,1)} %fusion.message_ref), custom_call_target="tpu_custom_call" | custom-call | flops 6442450944 | bytes 4718592 | tf_op jit(solution)/shard_map/pack/pallas_call | solution.py:73
  44.4 1.9 reduce.2
  46.2 0.7 all_to_all.26
  46.9 8.1 %all-to-all-done.3 = bf16[8,4,4,32,256]{4,3,2,0,1:T(8,128)(2,1)S(1)} async-done(((bf16[8,4,4,32,256]{4,3,2,0,1:T(8,128)(2,1)}), bf16[8,4,4,32,256]{4,3,2,0,1:T(8,128)(2,1)S(1)}, u32[]{:S(2)}, u32[]{:S(2)}) %all-to-all-start.3) | async-done | bytes 2097184 | tf_op jit(solution)/shard_map/all_to_all | solution.py:292
  55.0 5.7 %all-to-all-start = ((f32[32,1,96]{2,1,0:T(1,128)}), f32[32,1,96]{2,1,0:T(1,128)S(1)}, u32[]{:S(2)}, u32[]{:S(2)}) async-start(f32[32,1,96]{2,1,0:T(1,128)} %bitcast.3), calls=%async_computation | async-start | bytes 32768 | tf_op jit(solution)/shard_map/all_to_all | solution.py:284
  60.8 1.3 reduce_sum.24
  62.1 5.9 %all-to-all-done = f32[32,1,96]{2,1,0:T(1,128)S(1)} async-done(((f32[32,1,96]{2,1,0:T(1,128)}), f32[32,1,96]{2,1,0:T(1,128)S(1)}, u32[]{:S(2)}, u32[]{:S(2)}) %all-to-all-start) | async-done | bytes 12320 | tf_op jit(solution)/shard_map/all_to_all | solution.py:284
  67.9 18.2 %all_to_all.41 = bf16[8,4,32,256]{3,2,1,0:T(8,128)(2,1)S(1)} all-to-all(bf16[8,4,32,256]{3,2,1,0:T(8,128)(2,1)} %reduce_sum.24), channel_id=1, replica_groups=mesh['aa'=8,'ba'=4] {'aa'}, dimensions={0} | all-to-all | bytes 1048576 | tf_op jit(solution)/shard_map/all_to_all | solution.py:294
  86.1 2.7 %all-to-all-start.1 = ((bf16[32,96,256]{2,1,0:T(8,128)(2,1)}), bf16[32,96,256]{2,1,0:T(8,128)(2,1)S(1)}, u32[]{:S(2)}, u32[]{:S(2)}) async-start(bf16[32,96,256]{2,1,0:T(8,128)(2,1)} %bitcast.27), calls=%async_computation.1 | async-start | bytes 3145728 | tf_op jit(solution)/shard_map/all_to_all | solution.py:287
  88.9 0.0 all-gather.3.cloned.1.call-start
  88.9 0.1 reduce_sum.25
  89.0 8.0 %fusion.1 = bf16[4,32,1,256]{3,2,1,0:T(2,128)(2,1)S(1)} fusion(bf16[4,32,256,256]{3,2,1,0:T(8,128)(2,1)} %param.20, bf16[4,32,256,1]{2,1,0,3:T(8,128)(2,1)S(1)} %bitcast.31), kind=kOutput, calls=%fused_computation.3 | convolution fusion | flops 16777216 | bytes 16908288 | tf_op jit(solution)/shard_map/jmc,jmco->jmo/dot_general | solution.py:296
  97.1 7.7 %all_gather.9 = bf16[16,32,256]{2,1,0:T(8,128)(2,1)} all-gather(bf16[4,32,256]{2,1,0:T(8,128)(2,1)S(1)} %bitcast.32), channel_id=1, replica_groups=mesh['aa'=8,'ba'=4] {'ba'}, dimensions={0}, use_global_device_ids=true | all-gather | bytes 327680 | tf_op jit(solution)/shard_map/all_gather | solution.py:299
  104.7 0.0 all-gather.3.cloned.1.call-update
  104.8 0.5 broadcast.59
  105.3 0.7 reduce.8
  106.0 2.7 %reshape.26.column_ref = f32[3072,1]{1,0:T(8,128)} reshape(f32[32,96]{1,0:T(8,128)S(1)} %reduce.8) | data formatting | bytes 24576 | tf_op jit(solution)/shard_map/reshape | solution.py:121
  108.6 0.7 reshape.22.row_ref
  109.3 25.6 %all-to-all-done.1 = bf16[32,96,256]{2,1,0:T(8,128)(2,1)S(1)} async-done(((bf16[32,96,256]{2,1,0:T(8,128)(2,1)}), bf16[32,96,256]{2,1,0:T(8,128)(2,1)S(1)}, u32[]{:S(2)}, u32[]{:S(2)}) %all-to-all-start.1) | async-done | bytes 1572896 | tf_op jit(solution)/shard_map/all_to_all | solution.py:287
  134.9 0.0 copy-start.1
  134.9 1.2 copy-done.1
  136.1 11.4 %merge.1 = bf16[3072,256]{1,0:T(8,128)(2,1)} custom-call(f32[3072,1]{1,0:T(8,128)} %reshape.26.column_ref, f32[1,3072]{1,0:T(1,128)} %reshape.22.row_ref, bf16[3072,256]{1,0:T(8,128)(2,1)} %bitcast.28), custom_call_target="tpu_custom_call" | custom-call | flops 4831838208 | bytes 3145728 | tf_op jit(solution)/shard_map/merge/pallas_call | solution.py:107
  147.5 0.0 copy-start.5
  147.5 0.0 copy-start.4
  147.5 3.8 %all-to-all-start.2 = ((bf16[32,96,256]{2,1,0:T(8,128)(2,1)}), bf16[32,96,256]{2,1,0:T(8,128)(2,1)S(1)}, u32[]{:S(2)}, u32[]{:S(2)}) async-start(bf16[32,96,256]{2,1,0:T(8,128)(2,1)} %bitcast.30), calls=%async_computation.2 | async-start | bytes 3145728 | tf_op jit(solution)/shard_map/all_to_all | solution.py:303
  151.3 0.0 copy-start.7
  151.3 0.0 copy-start.6
  151.3 1.4 copy.37.z_ref
  152.7 0.0 copy-done.5
  152.7 1.3 copy.35.x_ref
  154.0 0.0 copy-done.4
  154.0 1.4 copy.36.y_ref
  155.4 0.0 copy-done.7
  155.4 1.3 copy.38.slots_ref
  156.7 0.0 copy-done.6
  156.7 1.5 copy.39.read_ref
  158.2 3.8 %all-gather.3.cloned.1.call-done = bf16[128,32,256]{2,1,0:T(8,128)(2,1)} async-done(((bf16[16,32,256]{2,1,0:T(8,128)(2,1)}), bf16[128,32,256]{2,1,0:T(8,128)(2,1)}) %all-gather.3.cloned.1.call-update) | async-done | bytes 2097168 | tf_op jit(solution)/shard_map/all_gather | solution.py:300
  162.0 12.9 %inverse.1.inverse_ref = f32[2048,256]{1,0:T(8,128)} custom-call(s32[2048,1]{1,0:T(8,128)} %copy.35.x_ref, s32[2048,1]{1,0:T(8,128)} %copy.36.y_ref, s32[2048,1]{1,0:T(8,128)} %copy.37.z_ref, bf16[128,256]{1,0:T(8,128)(2,1)} %constant.93.clone.tx_ref, bf16[128,16]{1,0:T(8,128)(2,1)} %constant.94.clone.ty_ref, bf16[128,256]{1,0:T(8,128)(2,1)} %constant.95.clone.tz_ref, ...), custom_call_target="tpu_custom_call" | custom-call | flops 4294967296 | bytes 2097152 | tf_op jit(solution)/shard_map/inverse/pallas_call | solution.py:198
  174.9 17.4 %all-to-all-done.2 = bf16[32,96,256]{2,1,0:T(8,128)(2,1)S(1)} async-done(((bf16[32,96,256]{2,1,0:T(8,128)(2,1)}), bf16[32,96,256]{2,1,0:T(8,128)(2,1)S(1)}, u32[]{:S(2)}, u32[]{:S(2)}) %all-to-all-start.2) | async-done | bytes 1572896 | tf_op jit(solution)/shard_map/all_to_all | solution.py:303
  192.3 0.0 copy-start.2
  192.3 1.1 copy-done.2
  193.4 12.0 %decode.1 = bf16[2048,256]{1,0:T(8,128)(2,1)} custom-call(s32[2048,1]{1,0:T(8,128)} %copy.38.slots_ref, bf16[3072,256]{1,0:T(8,128)(2,1)} %bitcast.29, f32[2048,256]{1,0:T(8,128)} %inverse.1.inverse_ref, f32[2048,1]{1,0:T(8,128)} %copy.39.read_ref, bf16[256,256]{1,0:T(8,128)(2,1)} %skip_ref.1, bf16[256,256]{1,0:T(8,128)(2,1)} %hidden_ref.1, ...), custom_call_target="tpu_custom_call" | custom-call | flops 3221225472 | bytes 3145728 | tf_op jit(solution)/shard_map/decode/pallas_call | solution.py:232
  (3 shorter events, 0.0 us)
Async XLA Ops:
  6.5 1.4 copy-start
  25.0 4.4 %copy-start.3 = (s32[2048]{0:T(1024)S(1)}, s32[2048]{0:T(1024)}, u32[]{:S(2)}) copy-start(s32[2048]{0:T(1024)} %get-tuple-element.13) | copy-start | bytes 24580
  25.0 30.1 %all-to-all-start.3 = ((bf16[8,4,4,32,256]{4,3,2,0,1:T(8,128)(2,1)}), bf16[8,4,4,32,256]{4,3,2,0,1:T(8,128)(2,1)S(1)}, u32[]{:S(2)}, u32[]{:S(2)}) async-start(bf16[8,4,4,32,256]{4,3,2,0,1:T(8,128)(2,1)} %copy.34), calls=%async_computation.3 | async-start | bytes 4194304 | tf_op jit(solution)/shard_map/all_to_all | solution.py:292
  55.0 12.9 %all-to-all-start = ((f32[32,1,96]{2,1,0:T(1,128)}), f32[32,1,96]{2,1,0:T(1,128)S(1)}, u32[]{:S(2)}, u32[]{:S(2)}) async-start(f32[32,1,96]{2,1,0:T(1,128)} %bitcast.3), calls=%async_computation | async-start | bytes 32768 | tf_op jit(solution)/shard_map/all_to_all | solution.py:284
  86.1 48.8 %all-to-all-start.1 = ((bf16[32,96,256]{2,1,0:T(8,128)(2,1)}), bf16[32,96,256]{2,1,0:T(8,128)(2,1)S(1)}, u32[]{:S(2)}, u32[]{:S(2)}) async-start(bf16[32,96,256]{2,1,0:T(8,128)(2,1)} %bitcast.27), calls=%async_computation.1 | async-start | bytes 3145728 | tf_op jit(solution)/shard_map/all_to_all | solution.py:287
  88.9 73.1 %all-gather.3.cloned.1.call-start = ((), (), s32[]{:S(2)}) async-start(), calls=%async_computation.5 | async-start | bytes 2359296 | tf_op jit(solution)/shard_map/all_gather | solution.py:300
  134.9 1.2 copy-start.1
  147.5 5.2 %copy-start.5 = (s32[2048]{0:T(1024)S(1)}, s32[2048]{0:T(1024)}, u32[]{:S(2)}) copy-start(s32[2048]{0:T(1024)} %get-tuple-element.12) | copy-start | bytes 24580
  147.5 6.5 %copy-start.4 = (s32[2048]{0:T(1024)S(1)}, s32[2048]{0:T(1024)}, u32[]{:S(2)}) copy-start(s32[2048]{0:T(1024)} %get-tuple-element.11) | copy-start | bytes 24580
  147.5 44.8 %all-to-all-start.2 = ((bf16[32,96,256]{2,1,0:T(8,128)(2,1)}), bf16[32,96,256]{2,1,0:T(8,128)(2,1)S(1)}, u32[]{:S(2)}, u32[]{:S(2)}) async-start(bf16[32,96,256]{2,1,0:T(8,128)(2,1)} %bitcast.30), calls=%async_computation.2 | async-start | bytes 3145728 | tf_op jit(solution)/shard_map/all_to_all | solution.py:303
  151.3 4.1 %copy-start.7 = (s32[1,2048]{1,0:T(1,128)S(1)}, s32[1,2048]{1,0:T(1,128)}, u32[]{:S(2)}) copy-start(s32[1,2048]{1,0:T(1,128)} %get-tuple-element.8) | copy-start | bytes 24580
  151.3 5.4 %copy-start.6 = (f32[2048]{0:T(1024)S(1)}, f32[2048]{0:T(1024)}, u32[]{:S(2)}) copy-start(f32[2048]{0:T(1024)} %param.17) | copy-start | bytes 24580
  192.3 1.1 copy-start.2
Sparse Core Ops, SparseCore 0:
  104.9 57.0 all-gather.2
where the time goes:
time: 213 us; the launch traced here: 212 us
  waiting for transfers between devices  60.8 us (29%)
  Pallas kernels  59.6 us (28%)
  blocking collectives  25.9 us (12%)
  local copies, waits for them, and re-layouts  20.1 us (9%)
  starting transfers between devices  16.6 us (8%)
  between operations  13.5 us (6%)
  matrix products  10.4 us (5%)
  other arithmetic  5.47 us (3%)
    all_to_all x1, waiting for transfers between devices, per_device(): lax.all_to_all(send_rows, axes, split_axis=0, concat_axis=0, tiled=True)  25.6 us
    all_to_all x1, blocking collectives, per_device(): lax.all_to_all(partial, 'aa', split_axis=0, concat_axis=0, tiled=True)  18.2 us
    all_to_all x1, waiting for transfers between devices, per_device(): lax.all_to_all(merged, axes, split_axis=0, concat_axis=0, tiled=True)  17.4 us
    pallas_call x1, Pallas kernels, inverse(): pl.pallas_call(functools.partial(inverse_kernel, modes), grid=(points //...  12.9 us
    pallas_call x1, Pallas kernels, decode(): pl.pallas_call(decode_kernel, grid=(points // block,), in_specs=[column,...  12 us
    pallas_call x1, Pallas kernels, pack(): pl.pallas_call(functools.partial(pack_kernel, devices, capacity), grid=(t...  11.8 us
    pallas_call x1, Pallas kernels, forward(): pl.pallas_call(forward_kernel, grid=(modes,), in_specs=[whole((1, points)...  11.5 us
    pallas_call x1, Pallas kernels, merge(): pl.pallas_call(merge_kernel, grid=(total // block,), in_specs=[pl.BlockSp...  11.4 us
  transfers between devices with their start and end apart: 5, of which 5 were waited for; matrix products, arithmetic and copies ran while one was open for 12% of the time, Pallas kernels for 17%

commit v1 on v0

v1 whole, which is shorter than its diff:
```python
import functools
import math

import jax
import jax.numpy as jnp
import numpy as np
from jax import lax
from jax.experimental import pallas as pl
from jax.experimental.pallas import tpu as pltpu
from jax.sharding import PartitionSpec as P

G = 64
LANES = 128
F32 = jnp.float32
BF16 = jnp.bfloat16
MESH = pl.DeviceIdType.MESH


def basis_np(modes, grid):
    k = np.arange(modes)[:, None]
    half = modes // 2
    freq = np.where(k < half, k, k - half + 1).astype(np.float64)
    phase = 2.0 * math.pi * freq * np.arange(grid)[None, :] / grid
    wave = np.where(k < half, np.cos(phase), np.sin(phase))
    norm = np.where(k == 0, math.sqrt(1.0 / grid), math.sqrt(2.0 / grid))
    return (wave * norm).astype(np.float32)


def split_table(table):
    high = table.astype(BF16)
    low = (table - high.astype(np.float32)).astype(BF16)
    return np.concatenate([high, low], axis=0)


def dot(a, b):
    return jnp.dot(a, b, preferred_element_type=F32)


def rows_of(block, *shape):
    if any(size % 16 for size in (block.shape[-2], shape[-2])):
        return block.astype(F32).reshape(shape).astype(BF16)
    return block.reshape(shape)


def hot_rows(values, points):
    lane = lax.broadcasted_iota(jnp.int32, (2 * G, points), 0) % G
    return (lane.astype(F32) == values).astype(F32).astype(BF16)


def hot_columns(values, points):
    lane = lax.broadcasted_iota(jnp.int32, (points, 2 * G), 1) % G
    return (lane.astype(F32) == values).astype(F32).astype(BF16)


def layer_kernel(
    sizes,
    info_ref, feat_ref, wm_ref, ws_ref, wh_ref, wo_ref, txr_ref, tyr_ref, tzr_ref, txc_ref, tyc_ref, tzc_ref,
    spec_hbm, out_ref,
    spec, slots, cols, message, plane, second, plane_c, second_c, total,
    send, recv, back, ret, wsend, wrecv, wrow,
    part, from_core, from_quad, quad, from_line, mixed, whole,
    spec_sem, where_s, where_r, rows_s, rows_r, ret_s, ret_r,
    core_s, core_r, quad_s, quad_r, line_s, line_r,
    gline_s, gline_r, gquad_s, gquad_r, gcore_s, gcore_r,
):
    na, nb, cap, modes_y, share = sizes
    n = na * nb
    naz, nbx = na // 2, nb // 2
    points, width = feat_ref.shape
    pairs = txr_ref.shape[0]
    modes = modes_y * nb
    a = lax.axis_index("aa")
    b = lax.axis_index("ba")
    me = a * nb + b
    az, ay, bx, bc = a // 2, a % 2, b // 2, b % 2

    def remote(src, dst, send_sem, recv_sem, to_a, to_b):
        return pltpu.make_async_remote_copy(
            src_ref=src, dst_ref=dst, send_sem=send_sem, recv_sem=recv_sem,
            device_id={"aa": to_a, "ba": to_b}, device_id_type=MESH,
        )

    spec_copy = pltpu.make_async_copy(spec_hbm, spec, spec_sem)
    spec_copy.start()
    barrier = pltpu.get_barrier_semaphore()

    def greet(k, _):
        peer = (me + k) % n
        pl.semaphore_signal(
            barrier, inc=1, device_id={"aa": peer // nb, "ba": peer % nb}, device_id_type=MESH
        )
        return 0

    lax.fori_loop(1, n, greet, 0)

    step = 256
    upper = (
        lax.broadcasted_iota(jnp.int32, (step, step), 0) <= lax.broadcasted_iota(jnp.int32, (step, step), 1)
    ).astype(F32).astype(BF16)
    carry = jnp.zeros((n, 1), F32)
    tile_at = lax.broadcasted_iota(jnp.int32, (n, step), 0).astype(F32)
    rank_at = lax.broadcasted_iota(jnp.int32, (LANES, step), 0).astype(F32)
    found = jnp.zeros((3 * n, LANES), F32)
    for start in range(0, points, step):
        piece = slice(start, start + step)
        tiles = info_ref[0:1, piece]
        hot = (tile_at == tiles).astype(F32)
        counts = dot(hot.astype(BF16), upper) + carry
        rank = jnp.sum(counts * hot, axis=0, keepdims=True) - 1.0
        slots[:, piece] = tiles * cap + rank
        carry = carry + jnp.sum(hot, axis=1, keepdims=True)
        marks = jnp.concatenate([hot * info_ref[1:2, piece], hot * info_ref[2:3, piece], hot], axis=0).astype(BF16)
        ranks = (rank_at == rank).astype(F32).astype(BF16)
        found = found + lax.dot_general(marks, ranks, (((1,), (1,)), ((), ())), preferred_element_type=F32)
    where = found[:n] * G + found[n : 2 * n] + (found[2 * n :] - 1.0)
    for tile in range(n):
        wsend[tile] = where[tile : tile + 1, :]
    for start in range(0, points, LANES):
        piece = slice(start, start + LANES)
        both = jnp.concatenate([slots[:, piece], info_ref[1:8, piece]], axis=0)
        cols[piece, :] = both.T

    message[...] = (cols[:, 6:7] * dot(feat_ref[...], wm_ref[...])).astype(BF16)

    pl.semaphore_wait(barrier, n - 1)

    group = nb * cap
    own = lax.broadcasted_iota(jnp.int32, (group, points), 0).astype(F32)

    def row_copy(src, dst, sem_s, sem_r, to_a, to_b):
        return remote(src.at[to_a * nb + to_b], dst.at[me], sem_s.at[to_a * nb + to_b], sem_r.at[me], to_a, to_b)

    def pack_step(i, _):
        to_a = (a + naz + i) % na
        base = (to_a * group).astype(F32)
        hot = (own == slots[...] - base).astype(F32).astype(BF16)
        rows = dot(hot, message[...])
        for to_b in range(nb):
            dest = to_a * nb + to_b
            send[dest] = rows[to_b * cap : (to_b + 1) * cap].astype(BF16)

            @pl.when(dest != me)
            def _():
                row_copy(wsend, wrecv, where_s, where_r, to_a, to_b).start()
                row_copy(send, recv, rows_s, rows_r, to_a, to_b).start()

        return 0

    lax.fori_loop(0, na, pack_step, 0)
    recv[me] = send[me]
    wrecv[me] = wsend[me]

    plane[...] = dot(txr_ref[...], hot_rows(info_ref[3:4, :], points)) * dot(
        tzr_ref[...], hot_rows(info_ref[5:6, :], points)
    )
    second[...] = dot(tyr_ref[...], hot_rows(info_ref[4:5, :], points))

    def forward(to_b):
        def one(jj, _):
            scaled = (plane[...] * second[pl.ds(to_b * modes_y + jj, 1), :]).astype(BF16)
            result = dot(scaled, message[...])
            part[to_b, jj] = result.reshape(2, naz, share, width).astype(BF16)
            return 0

        lax.fori_loop(0, modes_y, one, 0)

    def core_copy(to_x):
        return remote(
            part.at[to_x * 2 + (1 - bc)], from_core.at[to_x], core_s.at[to_x], core_r.at[to_x], a, bx * 2 + (1 - bc)
        )

    def quad_copy(kx, ky):
        to_x, to_y = (bx + kx) % nbx, (ay + ky) % 2
        k = kx * 2 + ky
        return remote(
            part.at[to_x * 2 + bc, :, to_y], from_quad.at[k], quad_s.at[k], quad_r.at[k],
            az * 2 + to_y, to_x * 2 + bc,
        )

    def line_copy(k):
        to_z = (az + k) % naz
        return remote(quad.at[:, to_z], from_line.at[k], line_s.at[k], line_r.at[k], to_z * 2 + ay, b)

    for kx in range(nbx):
        to_x = (bx + 1 + kx) % nbx
        forward(to_x * 2 + (1 - bc))
        core_copy(to_x).start()
    for kx in range(nbx):
        to_x = (bx + 1 + kx) % nbx
        forward(to_x * 2 + bc)
        core_copy(to_x).wait_recv()
        part[to_x * 2 + bc] = (part[to_x * 2 + bc].astype(F32) + from_core[to_x].astype(F32)).astype(BF16)
        for ky in (1, 0):
            k = (1 + kx) % nbx
            if (k, ky) != (0, 0):
                quad_copy(k, ky).start()

    plane_c[...] = dot(hot_columns(cols[:, 3:4], points), txc_ref[...]) * dot(
        hot_columns(cols[:, 5:6], points), tzc_ref[...]
    )
    second_c[...] = dot(hot_columns(cols[:, 4:5], points), tyc_ref[...])

    sums = part[b, :, ay].astype(F32)
    for kx in range(nbx):
        for ky in range(2):
            if (kx, ky) != (0, 0):
                quad_copy(kx, ky).wait_recv()
                sums = sums + from_quad[kx * 2 + ky].astype(F32)
    quad[...] = sums.astype(BF16)
    for k in range(1, naz):
        line_copy(k).start()
    spec_copy.wait()
    sums = quad[:, az].astype(F32)
    for k in range(1, naz):
        line_copy(k).wait_recv()
        sums = sums + from_line[k].astype(F32)
    mixed[...] = sums.reshape(modes_y * share, width)

    row_at = lax.broadcasted_iota(jnp.int32, (8, width), 0)

    def mix_step(i, _):
        rows = mixed[pl.ds(pl.multiple_of(i * 8, 8), 8), :].astype(BF16)
        out = jnp.zeros((8, width), F32)
        for r in range(8):
            out = jnp.where(row_at == r, dot(rows, spec[i * 8 + r]), out)
        mixed[pl.ds(pl.multiple_of(i * 8, 8), 8), :] = out
        return 0

    lax.fori_loop(0, modes_y * share // 8, mix_step, 0)
    whole[b, :, ay, az] = mixed[...].reshape(modes_y, share, width).astype(BF16)

    def gline_copy(k, at_z):
        to_z = (az + k) % naz
        here = whole.at[b, :, ay, at_z]
        return remote(here, here, gline_s.at[k], gline_r.at[k], to_z * 2 + ay, b)

    def gquad_copy(kx, ky, at_x, at_y):
        to_x, to_y = (bx + kx) % nbx, (ay + ky) % 2
        k = kx * 2 + ky
        here = whole.at[at_x * 2 + bc, :, at_y]
        return remote(here, here, gquad_s.at[k], gquad_r.at[k], az * 2 + to_y, to_x * 2 + bc)

    def gcore_copy(at_x, at_c):
        here = whole.at[at_x * 2 + at_c]
        return remote(here, here, gcore_s.at[at_x], gcore_r.at[at_x], a, bx * 2 + (1 - bc))

    for k in range(1, naz):
        gline_copy(k, az).start()

    def arrived(i, _):
        src = (me + i) % n
        row_copy(wsend, wrecv, where_s, where_r, src // nb, src % nb).wait_send()
        row_copy(send, recv, rows_s, rows_r, src // nb, src % nb).wait_send()
        remote(wsend.at[src], wrecv.at[src], where_s.at[src], where_r.at[src], src // nb, src % nb).wait_recv()
        remote(send.at[src], recv.at[src], rows_s.at[src], rows_r.at[src], src // nb, src % nb).wait_recv()
        return 0

    lax.fori_loop(1, n, arrived, 0)
    for tile in range(n):
        wrow[:, tile * cap : (tile + 1) * cap] = wrecv[tile][:, :cap]
    diagonal = lax.broadcasted_iota(jnp.int32, (cap, LANES), 0) == lax.broadcasted_iota(jnp.int32, (cap, LANES), 1)

    def merge_step(i, _):
        to_a = (a + naz + i) % na
        column = jnp.concatenate(
            [
                jnp.sum(jnp.where(diagonal, wrecv[to_a * nb + to_b], 0.0), axis=1, keepdims=True)
                for to_b in range(nb)
            ],
            axis=0,
        )
        same = (column == wrow[...]).astype(F32).astype(BF16)
        rows = dot(same, rows_of(recv[...], n * cap, width))
        for to_b in range(nb):
            dest = to_a * nb + to_b
            back[dest] = rows[to_b * cap : (to_b + 1) * cap].astype(BF16)

            @pl.when(dest != me)
            def _():
                row_copy(back, ret, ret_s, ret_r, to_a, to_b).start()

        return 0

    half = na // 2
    lax.fori_loop(0, half // 2, merge_step, 0)
    for k in range(1, naz):
        gline_copy(k, (az + naz - k) % naz).wait_recv()
    for kx in range(nbx):
        for ky in range(2):
            if (kx, ky) != (0, 0):
                gquad_copy(kx, ky, bx, ay).start()
    lax.fori_loop(half // 2, na, merge_step, 0)
    ret[me] = back[me]
    for kx in range(nbx):
        for ky in range(2):
            if (kx, ky) != (0, 0):
                gquad_copy(kx, ky, (bx + nbx - kx) % nbx, (ay + ky) % 2).wait_recv()
    for at_x in range(nbx):
        gcore_copy(at_x, bc).start()

    block = 256

    def inverse(at_b, first):
        part_b = rows_of(whole[at_b].reshape(modes_y, pairs // share, share, width), modes_y * pairs, width)

        def one(i, _):
            here = pl.ds(pl.multiple_of(i * block, block), block)
            base = plane_c[here, :]
            table = second_c[here, :]
            lane = lax.broadcasted_iota(jnp.int32, (block, modes), 1)
            scaled = []
            for jj in range(modes_y):
                factor = jnp.sum(jnp.where(lane == at_b * modes_y + jj, table, 0.0), axis=1, keepdims=True)
                scaled.append((base * factor).astype(BF16))
            value = dot(jnp.concatenate(scaled, axis=1), part_b)
            total[here, :] = value if first else total[here, :] + value
            return 0

        lax.fori_loop(0, points // block, one, 0)

    for at_x in range(nbx):
        inverse(at_x * 2 + bc, at_x == 0)
    for at_x in range(nbx):
        gcore_copy(at_x, 1 - bc).wait_recv()
        inverse(at_x * 2 + (1 - bc), False)

    def returned(i, _):
        src = (me + i) % n
        row_copy(back, ret, ret_s, ret_r, src // nb, src % nb).wait_send()
        remote(back.at[src], ret.at[src], ret_s.at[src], ret_r.at[src], src // nb, src % nb).wait_recv()
        return 0

    lax.fori_loop(1, n, returned, 0)

    def decode(i, _):
        here = pl.ds(pl.multiple_of(i * block, block), block)
        lane = lax.broadcasted_iota(jnp.int32, (block, n * cap), 1).astype(F32)
        hot = (lane == cols[here, 0:1]).astype(F32).astype(BF16)
        latent = dot(hot, rows_of(ret[...], n * cap, width)).astype(BF16)
        latent_out = jax.nn.gelu(total[here, :] + dot(latent, ws_ref[...])).astype(BF16)
        gathered = (cols[here, 7:8] * latent_out.astype(F32)).astype(BF16)
        hidden = jax.nn.gelu(dot(gathered, wh_ref[...])).astype(BF16)
        out_ref[here, :] = dot(hidden, wo_ref[...]).astype(BF16)
        return 0

    lax.fori_loop(0, points // block, decode, 0)

    for to_x in range(nbx):
        core_copy(to_x).wait_send()
        gcore_copy(to_x, bc).wait_send()
    for kx in range(nbx):
        for ky in range(2):
            if (kx, ky) != (0, 0):
                quad_copy(kx, ky).wait_send()
                gquad_copy(kx, ky, bx, ay).wait_send()
    for k in range(1, naz):
        line_copy(k).wait_send()
        gline_copy(k, az).wait_send()


def per_device(
    features,
    tile_ids,
    cell_ids,
    spread_weight,
    read_weight,
    message_weight,
    skip_weight,
    spectral_weight,
    hidden_weight,
    output_weight,
):
    points, width = features.shape
    na = lax.axis_size("aa")
    nb = lax.axis_size("ba")
    n = na * nb
    cap = 3 * points // (2 * n)
    tile_x = G // na
    tile_y = G // nb
    modes_y, share = spectral_weight.shape[0], spectral_weight.shape[1]
    modes = modes_y * nb
    pairs = share * na
    naz, nbx = na // 2, nb // 2

    order = np.arange(pairs).reshape(naz, 2, share).transpose(1, 0, 2).reshape(pairs)
    basis = basis_np(modes, G)
    tx = split_table(np.repeat(basis, modes, axis=0)[order].T)
    tz = split_table(np.tile(basis, (modes, 1))[order].T)
    ty = split_table(basis.T)
    tables = [jnp.asarray(np.ascontiguousarray(t.T)) for t in (tx, ty, tz)] + [jnp.asarray(t) for t in (tx, ty, tz)]

    targets = tile_ids[:, 0]
    high, low = cell_ids // G, cell_ids % G
    x = targets // nb * tile_x + cell_ids // (tile_y * G)
    y = targets % nb * tile_y + high % tile_y
    info = jnp.stack(
        [targets.astype(F32), high.astype(F32), low.astype(F32), x.astype(F32), y.astype(F32), low.astype(F32),
         spread_weight, read_weight]
    )
    spec = spectral_weight.reshape(modes_y * share, width, width)

    vmem = pl.BlockSpec(memory_space=pltpu.VMEM)
    dma = pltpu.SemaphoreType.DMA
    return pl.pallas_call(
        functools.partial(layer_kernel, (na, nb, cap, modes_y, share)),
        in_specs=[vmem] * 12 + [pl.BlockSpec(memory_space=pl.ANY)],
        out_specs=vmem,
        out_shape=jax.ShapeDtypeStruct((points, width), BF16),
        scratch_shapes=[
            pltpu.VMEM((modes_y * share, width, width), BF16),
            pltpu.VMEM((1, points), F32),
            pltpu.VMEM((points, 8), F32),
            pltpu.VMEM((points, width), BF16),
            pltpu.VMEM((pairs, points), F32),
            pltpu.VMEM((modes, points), F32),
            pltpu.VMEM((points, pairs), F32),
            pltpu.VMEM((points, modes), F32),
            pltpu.VMEM((points, width), F32),
            pltpu.VMEM((n, cap, width), BF16),
            pltpu.VMEM((n, cap, width), BF16),
            pltpu.VMEM((n, cap, width), BF16),
            pltpu.VMEM((n, cap, width), BF16),
            pltpu.VMEM((n, 1, LANES), F32),
            pltpu.VMEM((n, 1, LANES), F32),
            pltpu.VMEM((1, n * cap), F32),
            pltpu.VMEM((nb, modes_y, 2, naz, share, width), BF16),
            pltpu.VMEM((nbx, modes_y, 2, naz, share, width), BF16),
            pltpu.VMEM((2 * nbx, modes_y, naz, share, width), BF16),
            pltpu.VMEM((modes_y, naz, share, width), BF16),
            pltpu.VMEM((naz, modes_y, share, width), BF16),
            pltpu.VMEM((modes_y * share, width), F32),
            pltpu.VMEM((nb, modes_y, 2, naz, share, width), BF16),
            dma, dma((n,)), dma((n,)), dma((n,)), dma((n,)), dma((n,)), dma((n,)),
            dma((nbx,)), dma((nbx,)), dma((2 * nbx,)), dma((2 * nbx,)), dma((naz,)), dma((naz,)),
            dma((naz,)), dma((naz,)), dma((2 * nbx,)), dma((2 * nbx,)), dma((nbx,)), dma((nbx,)),
        ],
        compiler_params=pltpu.CompilerParams(
            collective_id=0, has_side_effects=True, vmem_limit_bytes=62 * 1024 * 1024
        ),
        name="layer",
    )(info, features, message_weight, skip_weight, hidden_weight, output_weight, *tables, spec)


def solution(mesh):
    placed = (
        P(("aa", "ba"), None),
        P(("aa", "ba"), None),
        P(("aa", "ba")),
        P(("aa", "ba")),
        P(("aa", "ba")),
        P(),
        P(),
        P("ba", "aa", None, None),
        P(),
        P(),
    )
    return jax.shard_map(
        per_device, mesh=mesh, in_specs=placed, out_specs=P(("aa", "ba"), None), check_vma=False
    )
```

time: 213 us -> 131 us (0.62)
  the two profiles are of different devices: /device:TPU:0 before, /device:TPU:28 now
where the time goes in v1:
time: 131 us
  Pallas kernels  126 us (96%)
  local copies, waits for them, and re-layouts  3.7 us (3%)
  other arithmetic  1.45 us (1%)
    pallas_call x1, Pallas kernels, per_device(): pl.pallas_call(functools.partial(layer_kernel, (na, nb, cap, modes_y, sha...  126 us

profile of v1, /device:TPU:28, one launch (start us, length us, event | category | flops | bytes accessed | tf_op | source)
XLA Modules:
  0.0 130.8 jit_solution(3825258352929913000)
XLA Ops:
  0.0 0.7 convert_bitcast_fusion
  0.7 0.7 fusion.7
  1.4 1.4 %stack.29.info_ref = f32[8,2048]{1,0:T(8,128)} concatenate(f32[1,2048]{1,0:T(1,128)S(1)} %convert_bitcast_fusion, f32[1,2048]{1,0:T(1,128)S(1)} %bitcast.15, f32[1,2048]{1,0:T(1,128)S(1)} %bitcast.11, f32[1,2048]{1,0:T(1,128)S(1)} %bitcast.14, f32[1,2048]{1,0:T(1,128)S(1)} %bitcast.13, f32[1,2048]{1,0:T(1,128)S(1)} %bitcast.12, f32[1,2048]{1,0:T(1,128)} %bitcast.17, ...), dimensions={0} | concatenate | bytes 131072 | tf_op jit(solution)/shard_map/stack | solution.py:396
  2.9 125.6 %layer.1 = bf16[2048,256]{1,0:T(8,128)(2,1)} custom-call(f32[8,2048]{1,0:T(8,128)} %stack.29.info_ref, bf16[2048,256]{1,0:T(8,128)(2,1)} %feat_ref.1, bf16[256,256]{1,0:T(8,128)(2,1)} %wm_ref.1, bf16[256,256]{1,0:T(8,128)(2,1)} %ws_ref.1, bf16[256,256]{1,0:T(8,128)(2,1)} %wh_ref.1, bf16[256,256]{1,0:T(8,128)(2,1)} %wo_ref.1, ...), custom_call_target="tpu_custom_call" | custom-call | tf_op jit(solution)/shard_map/layer/pallas_call | solution.py:404
  128.5 2.3 %copy.18 = bf16[2048,256]{1,0:T(8,128)(2,1)} copy(bf16[2048,256]{1,0:T(8,128)(2,1)} %layer.1) | data formatting | bytes 2097152

commit v2 on v1

v2 whole, which is shorter than its diff:
```python
import functools
import math

import jax
import jax.numpy as jnp
import numpy as np
from jax import lax
from jax.experimental import pallas as pl
from jax.experimental.pallas import tpu as pltpu
from jax.sharding import PartitionSpec as P

G = 64
LANES = 128
F32 = jnp.float32
BF16 = jnp.bfloat16
PACE = (4, 4, 0, 0, 18)
MESH = pl.DeviceIdType.MESH


def FAR(size):
    return [(size // 2 + i) % size for i in range(size) if (size // 2 + i) % size]


def basis_np(modes, grid):
    k = np.arange(modes)[:, None]
    half = modes // 2
    freq = np.where(k < half, k, k - half + 1).astype(np.float64)
    phase = 2.0 * math.pi * freq * np.arange(grid)[None, :] / grid
    wave = np.where(k < half, np.cos(phase), np.sin(phase))
    norm = np.where(k == 0, math.sqrt(1.0 / grid), math.sqrt(2.0 / grid))
    return (wave * norm).astype(np.float32)


def split_table(table):
    high = table.astype(BF16)
    low = (table - high.astype(np.float32)).astype(BF16)
    return np.concatenate([high, low], axis=0)


def dot(a, b):
    return jnp.dot(a, b, preferred_element_type=F32)


def rows_of(block, *shape):
    if any(size % 16 for size in (block.shape[-2], shape[-2])):
        return block.astype(F32).reshape(shape).astype(BF16)
    return block.reshape(shape)


def hot_rows(values, points):
    lane = lax.broadcasted_iota(jnp.int32, (2 * G, points), 0) % G
    return (lane.astype(F32) == values).astype(F32).astype(BF16)


def hot_columns(values, points):
    lane = lax.broadcasted_iota(jnp.int32, (points, 2 * G), 1) % G
    return (lane.astype(F32) == values).astype(F32).astype(BF16)


def layer_kernel(
    sizes,
    tile_ref, cell_ref, spread_ref, read_ref, feat_ref, wm_ref, ws_ref, wh_ref, txr_ref, tyr_ref, tzr_ref, txc_ref, tyc_ref, tzc_ref,
    spec_hbm, out_ref,
    spec, info, slots, cols, message, plane, second, plane_c, second_c, total, latent,
    send, recv, back, ret, wsend, wrecv, wrow,
    part, from_core, from_quad, quad, from_line, mixed, whole,
    spec_sem, where_s, where_r, rows_s, rows_r, ret_s, ret_r,
    core_s, core_r, quad_s, quad_r, line_s, line_r,
    gline_s, gline_r, gquad_s, gquad_r, gcore_s, gcore_r,
):
    na, nb, cap, modes_y, share = sizes
    n = na * nb
    naz, nbx = na // 2, nb // 2
    points, width = feat_ref.shape
    pairs = txr_ref.shape[0]
    modes = modes_y * nb
    a = lax.axis_index("aa")
    b = lax.axis_index("ba")
    me = a * nb + b
    az, ay, bx, bc = a // 2, a % 2, b // 2, b % 2
    turn = 1 - 2 * (az // (naz // 2))

    def remote(src, dst, send_sem, recv_sem, to_a, to_b):
        return pltpu.make_async_remote_copy(
            src_ref=src, dst_ref=dst, send_sem=send_sem, recv_sem=recv_sem,
            device_id={"aa": to_a, "ba": to_b}, device_id_type=MESH,
        )


    spec_copy = pltpu.make_async_copy(spec_hbm, spec, spec_sem)
    spec_copy.start()
    barrier = pltpu.get_barrier_semaphore()

    def greet(k, _):
        peer = (me + k) % n
        pl.semaphore_signal(
            barrier, inc=1, device_id={"aa": peer // nb, "ba": peer % nb}, device_id_type=MESH
        )
        return 0

    lax.fori_loop(1, n, greet, 0)


    tile = tile_ref[...].astype(F32)
    cell = cell_ref[...].astype(F32)
    tile_x, tile_y = G // na, G // nb
    row = jnp.floor((tile + 0.5) * (1.0 / nb))
    high = jnp.floor((cell + 0.5) * (1.0 / G))
    deep = jnp.floor((high + 0.5) * (1.0 / tile_y))
    low = cell - high * G
    info[0:1, :] = tile
    info[1:2, :] = high
    info[2:3, :] = low
    info[3:4, :] = row * tile_x + deep
    info[4:5, :] = (tile - row * nb) * tile_y + (high - deep * tile_y)
    info[5:6, :] = low
    info[6:7, :] = spread_ref[...]
    info[7:8, :] = read_ref[...]

    step = 256
    upper = (
        lax.broadcasted_iota(jnp.int32, (step, step), 0) <= lax.broadcasted_iota(jnp.int32, (step, step), 1)
    ).astype(F32).astype(BF16)
    carry = jnp.zeros((n, 1), F32)
    tile_at = lax.broadcasted_iota(jnp.int32, (n, step), 0).astype(F32)
    rank_at = lax.broadcasted_iota(jnp.int32, (LANES, step), 0).astype(F32)
    found = jnp.zeros((3 * n, LANES), F32)
    for start in range(0, points, step):
        piece = slice(start, start + step)
        tiles = info[0:1, piece]
        hot = (tile_at == tiles).astype(F32)
        counts = dot(hot.astype(BF16), upper) + carry
        rank = jnp.sum(counts * hot, axis=0, keepdims=True) - 1.0
        slots[:, piece] = tiles * cap + rank
        carry = carry + jnp.sum(hot, axis=1, keepdims=True)
        marks = jnp.concatenate([hot * info[1:2, piece], hot * info[2:3, piece], hot], axis=0).astype(BF16)
        ranks = (rank_at == rank).astype(F32).astype(BF16)
        found = found + lax.dot_general(marks, ranks, (((1,), (1,)), ((), ())), preferred_element_type=F32)
    where = found[:n] * G + found[n : 2 * n] + (found[2 * n :] - 1.0)
    for tile in range(n):
        wsend[tile] = where[tile : tile + 1, :]
    for start in range(0, points, LANES):
        piece = slice(start, start + LANES)
        both = jnp.concatenate([slots[:, piece], info[1:8, piece]], axis=0)
        cols[piece, :] = both.T

    message[...] = (cols[:, 6:7] * dot(feat_ref[...], wm_ref[...])).astype(BF16)


    pl.semaphore_wait(barrier, n - 1)


    block = 512

    group = nb * cap
    own = lax.broadcasted_iota(jnp.int32, (group, points), 0).astype(F32)

    def row_copy(src, dst, sem_s, sem_r, to_a, to_b):
        return remote(src.at[to_a * nb + to_b], dst.at[me], sem_s.at[to_a * nb + to_b], sem_r.at[me], to_a, to_b)

    def peer(dz, dy, dx, dc):
        return (az + turn * dz + naz) % naz * 2 + (ay + dy) % 2, (bx + dx) % nbx * 2 + (bc + dc) % 2

    def send_rows(to_a, to_b):
        row_copy(wsend, wrecv, where_s, where_r, to_a, to_b).start()
        row_copy(send, recv, rows_s, rows_r, to_a, to_b).start()

    def pack(dy):
        def one(i, _):
            dz = (naz // 2 + i) % naz
            to_a = (az + turn * dz + naz) % naz * 2 + (ay + dy) % 2
            base = (to_a * group).astype(F32)
            hot = (own == slots[...] - base).astype(F32).astype(BF16)
            rows = dot(hot, message[...])
            for to_b in range(nb):
                send[to_a * nb + to_b] = rows[to_b * cap : (to_b + 1) * cap].astype(BF16)
            if dy == 0:
                for dc in range(2):
                    to_b = bx * 2 + (bc + dc) % 2

                    @pl.when(to_a * nb + to_b != me)
                    def _():
                        send_rows(to_a, to_b)

            return 0

        lax.fori_loop(0, naz, one, 0)

    sides = [(dx, dy) for dx in range(nbx) for dy in range(2) if (dx, dy) != (0, 0)]
    far = [(dz, dy, dx, dc) for dz in FAR(naz) for dc in range(2) for dx, dy in sides]
    near = [(0, dy, dx, dc) for dc in range(2) for dx, dy in sides]
    pack(0)
    pack(1)
    for offsets in near:
        send_rows(*peer(*offsets))
    recv[me] = send[me]
    wrecv[me] = wsend[me]


    plane[...] = dot(txr_ref[...], hot_rows(info[3:4, :], points)) * dot(
        tzr_ref[...], hot_rows(info[5:6, :], points)
    )
    second[...] = dot(tyr_ref[...], hot_rows(info[4:5, :], points))

    def forward(to_b):
        def one(jj, _):
            scaled = (plane[...] * second[pl.ds(to_b * modes_y + jj, 1), :]).astype(BF16)
            result = dot(scaled, message[...])
            part[to_b, jj] = result.reshape(2, naz, share, width).astype(BF16)
            return 0

        lax.fori_loop(0, modes_y, one, 0)

    def core_copy(to_x):
        return remote(
            part.at[to_x * 2 + (1 - bc)], from_core.at[to_x], core_s.at[to_x], core_r.at[to_x], a, bx * 2 + (1 - bc)
        )

    def quad_copy(kx, ky):
        to_x, to_y = (bx + kx) % nbx, (ay + ky) % 2
        k = kx * 2 + ky
        return remote(
            part.at[to_x * 2 + bc, :, to_y], from_quad.at[k], quad_s.at[k], quad_r.at[k],
            az * 2 + to_y, to_x * 2 + bc,
        )

    def line_copy(k, inward=False):
        to_z = (az + turn * k + naz) % naz
        at_z = to_z if inward else az
        return remote(quad.at[:, to_z], from_line.at[at_z], line_s.at[to_z], line_r.at[at_z], to_z * 2 + ay, b)

    paced = iter(far)

    def pace(count):
        for offsets in [o for _, o in zip(range(count), paced)]:
            send_rows(*peer(*offsets))

    early = iter(PACE)
    for kx in range(nbx):
        to_x = (bx + 1 + kx) % nbx
        pace(len(far) * next(early) // 18)
        forward(to_x * 2 + (1 - bc))
        core_copy(to_x).start()
    for kx in range(nbx):
        to_x = (bx + 1 + kx) % nbx
        pace(len(far) * next(early) // 18)
        forward(to_x * 2 + bc)
        core_copy(to_x).wait_recv()
        part[to_x * 2 + bc] = (part[to_x * 2 + bc].astype(F32) + from_core[to_x].astype(F32)).astype(BF16)
        for ky in (1, 0):
            k = (1 + kx) % nbx
            if (k, ky) != (0, 0):
                quad_copy(k, ky).start()
    pace(len(far) * next(early) // 18)


    def position(i, _):
        here = pl.ds(pl.multiple_of(i * block, block), block)
        plane_c[here, :] = (
            dot(hot_columns(cols[here, 3:4], block), txc_ref[...])
            * dot(hot_columns(cols[here, 5:6], block), tzc_ref[...])
        ).astype(BF16)
        hot_y = hot_columns(cols[here, 4:5], block)
        for j in range(modes):
            second_c[j, here, :] = dot(hot_y, tyc_ref[j]).astype(BF16)
        return 0

    lax.fori_loop(0, points // block, position, 0)


    sums = part[b, :, ay].astype(F32)
    for kx in range(nbx):
        for ky in range(2):
            if (kx, ky) != (0, 0):
                quad_copy(kx, ky).wait_recv()
                sums = sums + from_quad[kx * 2 + ky].astype(F32)
    quad[...] = sums.astype(BF16)

    for k in FAR(naz):
        line_copy(k).start()
    pace(len(far))
    def gline_copy(k, inward=False):
        to_z = (az + turn * k + naz) % naz
        at_z = to_z if inward else az
        here = whole.at[b, :, ay, at_z]
        return remote(here, here, gline_s.at[to_z], gline_r.at[at_z], to_z * 2 + ay, b)

    def gquad_copy(kx, ky, at_x, at_y):
        to_x, to_y = (bx + kx) % nbx, (ay + ky) % 2
        k = kx * 2 + ky
        here = whole.at[at_x * 2 + bc, :, at_y]
        return remote(here, here, gquad_s.at[k], gquad_r.at[k], az * 2 + to_y, to_x * 2 + bc)

    def gcore_copy(k, at_x, at_y, at_c):
        here = whole.at[at_x * 2 + at_c, :, at_y]
        return remote(here, here, gcore_s.at[k], gcore_r.at[k], a, bx * 2 + (1 - bc))


    def arrived(i, _):
        src = (me + i) % n
        remote(wsend.at[src], wrecv.at[src], where_s.at[src], where_r.at[src], src // nb, src % nb).wait_recv()
        remote(send.at[src], recv.at[src], rows_s.at[src], rows_r.at[src], src // nb, src % nb).wait_recv()
        return 0

    lax.fori_loop(1, n, arrived, 0)

    for tile in range(n):
        wrow[:, tile * cap : (tile + 1) * cap] = wrecv[tile][:, :cap]
    diagonal = lax.broadcasted_iota(jnp.int32, (cap, LANES), 0) == lax.broadcasted_iota(jnp.int32, (cap, LANES), 1)

    def back_rows(to_a, to_b):
        row_copy(back, ret, ret_s, ret_r, to_a, to_b).start()

    def merge(dy, zero, count):
        def one(i, _):
            dz = (zero + i) % naz
            to_a = (az + turn * dz + naz) % naz * 2 + (ay + dy) % 2
            column = jnp.concatenate(
                [
                    jnp.sum(jnp.where(diagonal, wrecv[to_a * nb + to_b], 0.0), axis=1, keepdims=True)
                    for to_b in range(nb)
                ],
                axis=0,
            )
            same = (column == wrow[...]).astype(F32).astype(BF16)
            rows = dot(same, rows_of(recv[...], n * cap, width))
            for to_b in range(nb):
                back[to_a * nb + to_b] = rows[to_b * cap : (to_b + 1) * cap].astype(BF16)
            if dy == 0:
                for dc in range(2):
                    to_b = bx * 2 + (bc + dc) % 2

                    @pl.when(to_a * nb + to_b != me)
                    def _():
                        back_rows(to_a, to_b)

            return 0

        lax.fori_loop(0, count, one, 0)

    def far_back(first, last):
        for offsets in far[first:last]:
            back_rows(*peer(*offsets))

    merge(0, naz // 2, 1)
    merge(0, 0, 1)
    merge(1, 0, 1)
    for offsets in near:
        back_rows(*peer(*offsets))
    ret[me] = back[me]

    spec_copy.wait()
    sums = quad[:, az].astype(F32)
    for k in range(1, naz):
        line_copy(k, True).wait_recv()
        sums = sums + from_line[(az + turn * k + naz) % naz].astype(F32)
    mixed[...] = sums.reshape(modes_y * share, width)


    row_at = lax.broadcasted_iota(jnp.int32, (8, width), 0)

    def mix_step(i, _):
        rows = mixed[pl.ds(pl.multiple_of(i * 8, 8), 8), :].astype(BF16)
        out = jnp.zeros((8, width), F32)
        for r in range(8):
            out = jnp.where(row_at == r, dot(rows, spec[i * 8 + r]), out)
        mixed[pl.ds(pl.multiple_of(i * 8, 8), 8), :] = out
        return 0

    lax.fori_loop(0, modes_y * share // 8, mix_step, 0)
    whole[b, :, ay, az] = mixed[...].reshape(modes_y, share, width).astype(BF16)

    for k in FAR(naz):
        gline_copy(k).start()


    merge(0, naz // 2 + 1, naz - naz // 2 - 1)
    merge(0, 1, naz // 2 - 1)
    merge(1, 1, naz - 1)

    slab = 2 * nb

    def unpack(dz, first):

        at_z = (az + turn * dz + naz) % naz
        for q in range(slab):
            src = at_z * slab + q

            @pl.when(src != me)
            def _():
                remote(back.at[src], ret.at[src], ret_s.at[src], ret_r.at[src], src // nb, src % nb).wait_recv()


        rows = rows_of(ret[pl.ds(at_z * slab, slab)], slab * cap, width)
        base = (at_z * slab * cap).astype(F32)

        def one(i, _):
            here = pl.ds(pl.multiple_of(i * block, block), block)
            lane = lax.broadcasted_iota(jnp.int32, (block, slab * cap), 1).astype(F32) + base
            hot = (lane == cols[here, 0:1]).astype(F32).astype(BF16)
            value = dot(hot, rows)
            latent[here, :] = value if first else latent[here, :] + value
            return 0

        lax.fori_loop(0, points // block, one, 0)


    for k in range(1, naz):
        gline_copy(k, True).wait_recv()
    for kx in range(nbx):
        for ky in range(2):
            if (kx, ky) != (0, 0):
                gquad_copy(kx, ky, bx, ay).start()

    half = pairs // 2

    def inverse(at_b, at_y, first):
        part_b = rows_of(whole[at_b, :, at_y].reshape(modes_y, naz * share, width), modes_y * half, width)

        def one(i, _):
            here = pl.ds(pl.multiple_of(i * block, block), block)
            base = plane_c[here, pl.ds(pl.multiple_of(at_y * half, half), half)]
            scaled = [base * second_c[at_b * modes_y + jj, here, :] for jj in range(modes_y)]
            value = dot(jnp.concatenate(scaled, axis=1), part_b)
            total[here, :] = value if first else total[here, :] + value
            return 0

        lax.fori_loop(0, points // block, one, 0)

    def take(kx, ky):
        at_x, at_y = (bx + nbx - kx) % nbx, (ay + ky) % 2
        first = (kx, ky) == (0, 0)
        if not first:

            gquad_copy(kx, ky, at_x, at_y).wait_recv()

        gcore_copy(kx * 2 + ky, at_x, at_y, bc).start()
        inverse(at_x * 2 + bc, at_y, first)
        if first:
            far_back(0, len(far) // 3)

        gcore_copy(kx * 2 + ky, at_x, at_y, 1 - bc).wait_recv()

        inverse(at_x * 2 + (1 - bc), at_y, False)
        if first:
            far_back(len(far) // 3, len(far))

    take(0, 0)
    for dz in [0] + FAR(naz):

        unpack(dz, dz == 0)
    for dx, dy in sides:
        take(dx, dy)

    def left(i, _):
        src = (me + i) % n
        row_copy(back, ret, ret_s, ret_r, src // nb, src % nb).wait_send()
        row_copy(wsend, wrecv, where_s, where_r, src // nb, src % nb).wait_send()
        row_copy(send, recv, rows_s, rows_r, src // nb, src % nb).wait_send()
        return 0

    lax.fori_loop(1, n, left, 0)


    def decode(i, _):
        here = pl.ds(pl.multiple_of(i * block, block), block)
        latent_out = jax.nn.gelu(total[here, :] + dot(latent[here, :].astype(BF16), ws_ref[...])).astype(BF16)
        gathered = (cols[here, 7:8] * latent_out.astype(F32)).astype(BF16)
        out_ref[here, :] = jax.nn.gelu(dot(gathered, wh_ref[...])).astype(BF16)
        return 0

    lax.fori_loop(0, points // block, decode, 0)


    for to_x in range(nbx):
        core_copy(to_x).wait_send()
    for kx in range(nbx):
        for ky in range(2):
            gcore_copy(kx * 2 + ky, bx, ay, bc).wait_send()
            if (kx, ky) != (0, 0):
                quad_copy(kx, ky).wait_send()
                gquad_copy(kx, ky, bx, ay).wait_send()
    for k in range(1, naz):
        line_copy(k).wait_send()
        gline_copy(k).wait_send()


def per_device(
    features,
    tile_ids,
    cell_ids,
    spread_weight,
    read_weight,
    message_weight,
    skip_weight,
    spectral_weight,
    hidden_weight,
    output_weight,
):
    points, width = features.shape
    na = lax.axis_size("aa")
    nb = lax.axis_size("ba")
    n = na * nb
    cap = 3 * points // (2 * n)
    modes_y, share = spectral_weight.shape[0], spectral_weight.shape[1]
    modes = modes_y * nb
    pairs = share * na
    naz, nbx = na // 2, nb // 2

    order = np.arange(pairs).reshape(naz, 2, share).transpose(1, 0, 2).reshape(pairs)
    basis = basis_np(modes, G)
    tx = split_table(np.repeat(basis, modes, axis=0)[order].T)
    tz = split_table(np.tile(basis, (modes, 1))[order].T)
    ty = split_table(basis.T)
    tables = [jnp.asarray(np.ascontiguousarray(t.T)) for t in (tx, ty, tz)] + [
        jnp.asarray(t) for t in (tx, np.repeat(ty.T[:, :, None], pairs // 2, axis=2), tz)
    ]

    spec = spectral_weight.reshape(modes_y * share, width, width)

    vmem = pl.BlockSpec(memory_space=pltpu.VMEM)
    dma = pltpu.SemaphoreType.DMA
    hidden = pl.pallas_call(
        functools.partial(layer_kernel, (na, nb, cap, modes_y, share)),
        in_specs=[vmem] * 14 + [pl.BlockSpec(memory_space=pl.ANY)],
        out_specs=vmem,
        out_shape=jax.ShapeDtypeStruct((points, width), BF16),
        scratch_shapes=[
            pltpu.VMEM((modes_y * share, width, width), BF16),
            pltpu.VMEM((8, points), F32),
            pltpu.VMEM((1, points), F32),
            pltpu.VMEM((points, 8), F32),
            pltpu.VMEM((points, width), BF16),
            pltpu.VMEM((pairs, points), F32),
            pltpu.VMEM((modes, points), F32),
            pltpu.VMEM((points, pairs), BF16),
            pltpu.VMEM((modes, points, pairs // 2), BF16),
            pltpu.VMEM((points, width), F32),
            pltpu.VMEM((points, width), F32),
            pltpu.VMEM((n, cap, width), BF16),
            pltpu.VMEM((n, cap, width), BF16),
            pltpu.VMEM((n, cap, width), BF16),
            pltpu.VMEM((n, cap, width), BF16),
            pltpu.VMEM((n, 1, LANES), F32),
            pltpu.VMEM((n, 1, LANES), F32),
            pltpu.VMEM((1, n * cap), F32),
            pltpu.VMEM((nb, modes_y, 2, naz, share, width), BF16),
            pltpu.VMEM((nbx, modes_y, 2, naz, share, width), BF16),
            pltpu.VMEM((2 * nbx, modes_y, naz, share, width), BF16),
            pltpu.VMEM((modes_y, naz, share, width), BF16),
            pltpu.VMEM((naz, modes_y, share, width), BF16),
            pltpu.VMEM((modes_y * share, width), F32),
            pltpu.VMEM((nb, modes_y, 2, naz, share, width), BF16),
            dma, dma((n,)), dma((n,)), dma((n,)), dma((n,)), dma((n,)), dma((n,)),
            dma((nbx,)), dma((nbx,)), dma((2 * nbx,)), dma((2 * nbx,)), dma((naz,)), dma((naz,)),
            dma((naz,)), dma((naz,)), dma((2 * nbx,)), dma((2 * nbx,)), dma((2 * nbx,)), dma((2 * nbx,)),
        ],
        compiler_params=pltpu.CompilerParams(
            collective_id=0, has_side_effects=True, vmem_limit_bytes=62 * 1024 * 1024
        ),
        name="layer",
    )(
        tile_ids.reshape(1, points), cell_ids.reshape(1, points), spread_weight.reshape(1, points),
        read_weight.reshape(1, points), features, message_weight, skip_weight, hidden_weight, *tables, spec,
    )
    return dot(hidden, output_weight).astype(BF16)


def solution(mesh):
    placed = (
        P(("aa", "ba"), None),
        P(("aa", "ba"), None),
        P(("aa", "ba")),
        P(("aa", "ba")),
        P(("aa", "ba")),
        P(),
        P(),
        P("ba", "aa", None, None),
        P(),
        P(),
    )
    return jax.shard_map(
        per_device, mesh=mesh, in_specs=placed, out_specs=P(("aa", "ba"), None), check_vma=False
    )
```

time: 131 us -> 109 us (0.83)
  the two profiles are of different devices: /device:TPU:28 before, /device:TPU:0 now
where the time goes in v2:
time: 109 us; the launch traced here: 108 us
  Pallas kernels  105 us (96%)
  matrix products  2.62 us (2%)
    pallas_call x1, Pallas kernels, per_device(): pl.pallas_call(functools.partial(layer_kernel, (na, nb, cap, modes_y, sha...  105 us
    dot_general x1, matrix products, dot(): return jnp.dot(a, b, preferred_element_type=F32)  2.62 us

profile of v2, /device:TPU:0, one launch (start us, length us, event | category | flops | bytes accessed | tf_op | source)
XLA Modules:
  0.0 107.9 jit_solution(16566648642289015319)
XLA Ops:
  0.0 0.0 copy-start
  0.0 105.3 %layer.1 = bf16[2048,256]{1,0:T(8,128)(2,1)} custom-call(s32[1,2048]{1,0:T(1,128)} %bitcast.8, s32[1,2048]{1,0:T(1,128)} %bitcast.9, f32[1,2048]{1,0:T(1,128)} %bitcast.10, f32[1,2048]{1,0:T(1,128)} %bitcast.11, bf16[2048,256]{1,0:T(8,128)(2,1)} %feat_ref.1, bf16[256,256]{1,0:T(8,128)(2,1)} %wm_ref.1, bf16[256,256]{1,0:T(8,128)(2,1)} %ws_ref.1, ...), custom_call_target="tpu_custom_call" | custom-call | tf_op jit(solution)/shard_map/layer/pallas_call | solution.py:523
  105.3 0.0 copy-done
  105.3 2.6 %convolution_convert_fusion = bf16[2048,256]{1,0:T(8,128)(2,1)} fusion(bf16[2048,256]{1,0:T(8,128)(2,1)} %layer.1, bf16[256,256]{1,0:T(8,128)(2,1)S(1)} %copy-done), kind=kOutput, calls=%fused_computation | convolution fusion | flops 268959744 | bytes 2228224 | tf_op jit(solution)/shard_map/dot_general | solution.py:41
Async XLA Ops:
  0.0 105.3 %copy-start = (bf16[256,256]{1,0:T(8,128)(2,1)S(1)}, bf16[256,256]{1,0:T(8,128)(2,1)}, u32[]{:S(2)}) copy-start(bf16[256,256]{1,0:T(8,128)(2,1)} %param.25) | copy-start | bytes 393220

commit v3 on v2

--- a/solution.py
+++ b/solution.py
@@ -59,14 +59,15 @@
 
 def layer_kernel(
     sizes,
-    tile_ref, cell_ref, spread_ref, read_ref, feat_ref, wm_ref, ws_ref, wh_ref, txr_ref, tyr_ref, tzr_ref, txc_ref, tyc_ref, tzc_ref,
+    tile_hbm, cell_hbm, spread_hbm, read_hbm, feat_hbm, wm_hbm, ws_hbm, wh_hbm, txr_hbm, tyr_hbm, tzr_hbm, txc_hbm, tyc_hbm, tzc_hbm,
     spec_hbm, out_ref,
     spec, info, slots, cols, message, plane, second, plane_c, second_c, total, latent,
     send, recv, back, ret, wsend, wrecv, wrow,
     part, from_core, from_quad, quad, from_line, mixed, whole,
     spec_sem, where_s, where_r, rows_s, rows_r, ret_s, ret_r,
     core_s, core_r, quad_s, quad_r, line_s, line_r,
-    gline_s, gline_r, gquad_s, gquad_r, gcore_s, gcore_r,
+    gline_s, gline_r, gquad_s, gquad_r, gcore_s, gcore_r, load_sem,
+    tile_ref, cell_ref, spread_ref, read_ref, feat_ref, wm_ref, ws_ref, wh_ref, txr_ref, tyr_ref, tzr_ref, txc_ref, tyc_ref, tzc_ref,
 ):
     na, nb, cap, modes_y, share = sizes
     n = na * nb
@@ -87,8 +88,14 @@
         )
 
 
-    spec_copy = pltpu.make_async_copy(spec_hbm, spec, spec_sem)
-    spec_copy.start()
+    loads = [
+        pltpu.make_async_copy(src, dst, load_sem.at[i])
+        for i, (src, dst) in enumerate([
+            (tile_hbm, tile_ref), (cell_hbm, cell_ref), (spread_hbm, spread_ref), (read_hbm, read_ref),
+            (feat_hbm, feat_ref), (wm_hbm, wm_ref), (ws_hbm, ws_ref), (wh_hbm, wh_ref), (txr_hbm, txr_ref),
+            (tyr_hbm, tyr_ref), (tzr_hbm, tzr_ref), (txc_hbm, txc_ref), (tyc_hbm, tyc_ref), (tzc_hbm, tzc_ref),
+        ])
+    ]
     barrier = pltpu.get_barrier_semaphore()
 
     def greet(k, _):
@@ -99,8 +106,14 @@
         return 0
 
     lax.fori_loop(1, n, greet, 0)
-
-
+    for load in loads:
+        load.start()
+    spec_copy = pltpu.make_async_copy(spec_hbm, spec, spec_sem)
+    spec_copy.start()
+
+
+    for load in loads[:4]:
+        load.wait()
     tile = tile_ref[...].astype(F32)
     cell = cell_ref[...].astype(F32)
     tile_x, tile_y = G // na, G // nb
@@ -144,6 +157,8 @@
         both = jnp.concatenate([slots[:, piece], info[1:8, piece]], axis=0)
         cols[piece, :] = both.T
 
+    for load in loads[4:]:
+        load.wait()
     message[...] = (cols[:, 6:7] * dot(feat_ref[...], wm_ref[...])).astype(BF16)
 
 
@@ -175,12 +190,11 @@
             for to_b in range(nb):
                 send[to_a * nb + to_b] = rows[to_b * cap : (to_b + 1) * cap].astype(BF16)
             if dy == 0:
-                for dc in range(2):
-                    to_b = bx * 2 + (bc + dc) % 2
-
-                    @pl.when(to_a * nb + to_b != me)
-                    def _():
-                        send_rows(to_a, to_b)
+
+                @pl.when(to_a != a)
+                def _():
+                    for dc in range(2):
+                        send_rows(to_a, bx * 2 + (bc + dc) % 2)
 
             return 0
 
@@ -193,6 +207,13 @@
     pack(1)
     for offsets in near:
         send_rows(*peer(*offsets))
+    send_rows(a, bx * 2 + 1 - bc)
+
+    @pl.when(bc == 1)
+    def _():
+        for offsets in far:
+            send_rows(*peer(*offsets))
+
     recv[me] = send[me]
     wrecv[me] = wsend[me]
 
@@ -229,21 +250,12 @@
         at_z = to_z if inward else az
         return remote(quad.at[:, to_z], from_line.at[at_z], line_s.at[to_z], line_r.at[at_z], to_z * 2 + ay, b)
 
-    paced = iter(far)
-
-    def pace(count):
-        for offsets in [o for _, o in zip(range(count), paced)]:
-            send_rows(*peer(*offsets))
-
-    early = iter(PACE)
     for kx in range(nbx):
         to_x = (bx + 1 + kx) % nbx
-        pace(len(far) * next(early) // 18)
         forward(to_x * 2 + (1 - bc))
         core_copy(to_x).start()
     for kx in range(nbx):
         to_x = (bx + 1 + kx) % nbx
-        pace(len(far) * next(early) // 18)
         forward(to_x * 2 + bc)
         core_copy(to_x).wait_recv()
         part[to_x * 2 + bc] = (part[to_x * 2 + bc].astype(F32) + from_core[to_x].astype(F32)).astype(BF16)
@@ -251,7 +263,6 @@
             k = (1 + kx) % nbx
             if (k, ky) != (0, 0):
                 quad_copy(k, ky).start()
-    pace(len(far) * next(early) // 18)
 
 
     def position(i, _):
@@ -267,6 +278,11 @@
 
     lax.fori_loop(0, points // block, position, 0)
 
+    @pl.when(bc == 0)
+    def _():
+        for offsets in far[: len(far) // 3]:
+            send_rows(*peer(*offsets))
+
 
     sums = part[b, :, ay].astype(F32)
     for kx in range(nbx):
@@ -278,7 +294,12 @@
 
     for k in FAR(naz):
         line_copy(k).start()
-    pace(len(far))
+
+    @pl.when(bc == 0)
+    def _():
+        for offsets in far[len(far) // 3 :]:
+            send_rows(*peer(*offsets))
+
     def gline_copy(k, inward=False):
         to_z = (az + turn * k + naz) % naz
         at_z = to_z if inward else az
@@ -294,6 +315,31 @@
     def gcore_copy(k, at_x, at_y, at_c):
         here = whole.at[at_x * 2 + at_c, :, at_y]
         return remote(here, here, gcore_s.at[k], gcore_r.at[k], a, bx * 2 + (1 - bc))
+
+
+    spec_copy.wait()
+    sums = quad[:, az].astype(F32)
+    for k in range(1, naz):
+        line_copy(k, True).wait_recv()
+        sums = sums + from_line[(az + turn * k + naz) % naz].astype(F32)
+    mixed[...] = sums.reshape(modes_y * share, width)
+
+
+    row_at = lax.broadcasted_iota(jnp.int32, (8, width), 0)
+
+    def mix_step(i, _):
+        rows = mixed[pl.ds(pl.multiple_of(i * 8, 8), 8), :].astype(BF16)
+        out = jnp.zeros((8, width), F32)
+        for r in range(8):
+            out = jnp.where(row_at == r, dot(rows, spec[i * 8 + r]), out)
+        mixed[pl.ds(pl.multiple_of(i * 8, 8), 8), :] = out
+        return 0
+
+    lax.fori_loop(0, modes_y * share // 8, mix_step, 0)
+    whole[b, :, ay, az] = mixed[...].reshape(modes_y, share, width).astype(BF16)
+
+    for k in FAR(naz):
+        gline_copy(k).start()
 
 
     def arrived(i, _):
@@ -348,36 +394,6 @@
     for offsets in near:
         back_rows(*peer(*offsets))
     ret[me] = back[me]
-
-    spec_copy.wait()
-    sums = quad[:, az].astype(F32)
-    for k in range(1, naz):
-        line_copy(k, True).wait_recv()
-        sums = sums + from_line[(az + turn * k + naz) % naz].astype(F32)
-    mixed[...] = sums.reshape(modes_y * share, width)
-
-
-    row_at = lax.broadcasted_iota(jnp.int32, (8, width), 0)
-
-    def mix_step(i, _):
-        rows = mixed[pl.ds(pl.multiple_of(i * 8, 8), 8), :].astype(BF16)
-        out = jnp.zeros((8, width), F32)
-        for r in range(8):
-            out = jnp.where(row_at == r, dot(rows, spec[i * 8 + r]), out)
-        mixed[pl.ds(pl.multiple_of(i * 8, 8), 8), :] = out
-        return 0
-
-    lax.fori_loop(0, modes_y * share // 8, mix_step, 0)
-    whole[b, :, ay, az] = mixed[...].reshape(modes_y, share, width).astype(BF16)
-
-    for k in FAR(naz):
-        gline_copy(k).start()
-
-
-    merge(0, naz // 2 + 1, naz - naz // 2 - 1)
-    merge(0, 1, naz // 2 - 1)
-    merge(1, 1, naz - 1)
-
     slab = 2 * nb
 
     def unpack(dz, first):
@@ -412,6 +428,11 @@
             if (kx, ky) != (0, 0):
                 gquad_copy(kx, ky, bx, ay).start()
 
+
+    merge(0, naz // 2 + 1, naz - naz // 2 - 1)
+    merge(0, 1, naz // 2 - 1)
+    merge(1, 1, naz - 1)
+
     half = pairs // 2
 
     def inverse(at_b, at_y, first):
@@ -446,11 +467,12 @@
             far_back(len(far) // 3, len(far))
 
     take(0, 0)
-    for dz in [0] + FAR(naz):
-
-        unpack(dz, dz == 0)
-    for dx, dy in sides:
-        take(dx, dy)
+    unpack(0, True)
+    quarters = [(kx, ky) for kx in range(nbx) for ky in range(2)][1:]
+    for kx, ky in quarters:
+        take(kx, ky)
+    for dz in FAR(naz):
+        unpack(dz, False)
 
     def left(i, _):
         src = (me + i) % n
@@ -518,13 +540,17 @@
 
     spec = spectral_weight.reshape(modes_y * share, width, width)
 
+    inputs = [
+        tile_ids.reshape(1, points), cell_ids.reshape(1, points), spread_weight.reshape(1, points),
+        read_weight.reshape(1, points), features, message_weight, skip_weight, hidden_weight, *tables,
+    ]
     vmem = pl.BlockSpec(memory_space=pltpu.VMEM)
     dma = pltpu.SemaphoreType.DMA
     hidden = pl.pallas_call(
         functools.partial(layer_kernel, (na, nb, cap, modes_y, share)),
-        in_specs=[vmem] * 14 + [pl.BlockSpec(memory_space=pl.ANY)],
+        in_specs=[pl.BlockSpec(memory_space=pl.ANY)] * (len(inputs) + 1),
         out_specs=vmem,
-        out_shape=jax.ShapeDtypeStruct((points, width), BF16),
+        out_shape=pltpu.VMEM((points, width), BF16),
         scratch_shapes=[
             pltpu.VMEM((modes_y * share, width, width), BF16),
             pltpu.VMEM((8, points), F32),
@@ -554,15 +580,13 @@
             dma, dma((n,)), dma((n,)), dma((n,)), dma((n,)), dma((n,)), dma((n,)),
             dma((nbx,)), dma((nbx,)), dma((2 * nbx,)), dma((2 * nbx,)), dma((naz,)), dma((naz,)),
             dma((naz,)), dma((naz,)), dma((2 * nbx,)), dma((2 * nbx,)), dma((2 * nbx,)), dma((2 * nbx,)),
-        ],
+            dma((len(inputs),)),
+        ] + [pltpu.VMEM(value.shape, value.dtype) for value in inputs],
         compiler_params=pltpu.CompilerParams(
-            collective_id=0, has_side_effects=True, vmem_limit_bytes=62 * 1024 * 1024
+            collective_id=0, has_side_effects=True, vmem_limit_bytes=56 * 1024 * 1024
         ),
         name="layer",
-    )(
-        tile_ids.reshape(1, points), cell_ids.reshape(1, points), spread_weight.reshape(1, points),
-        read_weight.reshape(1, points), features, message_weight, skip_weight, hidden_weight, *tables, spec,
-    )
+    )(*inputs, spec)
     return dot(hidden, output_weight).astype(BF16)
 
 

time: 109 us -> 101 us (0.927); the launches traced: 108 us -> 101 us
  Pallas kernels: 105 us -> 99.7 us
  matrix products: 2.62 us -> 1.41 us
    pallas_call x1, Pallas kernels: 105 us -> 99.7 us  [per_device(): pl.pallas_call(functools.partial(layer_kernel, (na, nb, cap, modes_y, sha...]
    dot_general x1, matrix products: 2.62 us -> 1.41 us  [dot(): return jnp.dot(a, b, preferred_element_type=F32)]
where the time goes in v3:
time: 101 us
  Pallas kernels  99.7 us (99%)
  matrix products  1.41 us (1%)
    pallas_call x1, Pallas kernels, per_device(): pl.pallas_call(functools.partial(layer_kernel, (na, nb, cap, modes_y, sha...  99.7 us

profile of v3, /device:TPU:0, one launch (start us, length us, event | category | flops | bytes accessed | tf_op | source)
XLA Modules:
  0.0 101.1 jit_solution(5013366168598973475)
XLA Ops:
  0.0 0.0 copy-start
  0.0 99.7 %layer.1 = bf16[2048,256]{1,0:T(8,128)(2,1)S(1)} custom-call(s32[1,2048]{1,0:T(1,128)} %bitcast.8, s32[1,2048]{1,0:T(1,128)} %bitcast.9, f32[1,2048]{1,0:T(1,128)} %bitcast.10, f32[1,2048]{1,0:T(1,128)} %bitcast.11, bf16[2048,256]{1,0:T(8,128)(2,1)} %feat_hbm.1, bf16[256,256]{1,0:T(8,128)(2,1)} %wm_hbm.1, bf16[256,256]{1,0:T(8,128)(2,1)} %ws_hbm.1, ...), custom_call_target="tpu_custom_call" | custom-call | tf_op jit(solution)/shard_map/layer/pallas_call | solution.py:549
  99.7 0.0 copy-done
  99.7 1.4 %convolution_convert_fusion = bf16[2048,256]{1,0:T(8,128)(2,1)} fusion(bf16[2048,256]{1,0:T(8,128)(2,1)S(1)} %layer.1, bf16[256,256]{1,0:T(8,128)(2,1)S(1)} %copy-done), kind=kOutput, calls=%fused_computation | convolution fusion | flops 268959744 | bytes 2228224 | tf_op jit(solution)/shard_map/dot_general | solution.py:41
Async XLA Ops:
  0.0 99.7 %copy-start = (bf16[256,256]{1,0:T(8,128)(2,1)S(1)}, bf16[256,256]{1,0:T(8,128)(2,1)}, u32[]{:S(2)}) copy-start(bf16[256,256]{1,0:T(8,128)(2,1)} %param.25) | copy-start | bytes 393220

commit v4 on v3

--- a/solution.py
+++ b/solution.py
@@ -165,7 +165,7 @@
     pl.semaphore_wait(barrier, n - 1)
 
 
-    block = 512
+    block = 1024
 
     group = nb * cap
     own = lax.broadcasted_iota(jnp.int32, (group, points), 0).astype(F32)
@@ -280,7 +280,7 @@
 
     @pl.when(bc == 0)
     def _():
-        for offsets in far[: len(far) // 3]:
+        for offsets in far[: len(far) * 8 // 18]:
             send_rows(*peer(*offsets))
 
 
@@ -297,7 +297,7 @@
 
     @pl.when(bc == 0)
     def _():
-        for offsets in far[len(far) // 3 :]:
+        for offsets in far[len(far) * 8 // 18 :]:
             send_rows(*peer(*offsets))
 
     def gline_copy(k, inward=False):
@@ -396,7 +396,7 @@
     ret[me] = back[me]
     slab = 2 * nb
 
-    def unpack(dz, first):
+    def unpack(dz, first, last=False):
 
         at_z = (az + turn * dz + naz) % naz
         for q in range(slab):
@@ -415,7 +415,13 @@
             lane = lax.broadcasted_iota(jnp.int32, (block, slab * cap), 1).astype(F32) + base
             hot = (lane == cols[here, 0:1]).astype(F32).astype(BF16)
             value = dot(hot, rows)
-            latent[here, :] = value if first else latent[here, :] + value
+            value = value if first else latent[here, :] + value
+            if not last:
+                latent[here, :] = value
+                return 0
+            latent_out = jax.nn.gelu(total[here, :] + dot(value.astype(BF16), ws_ref[...])).astype(BF16)
+            gathered = (cols[here, 7:8] * latent_out.astype(F32)).astype(BF16)
+            out_ref[here, :] = jax.nn.gelu(dot(gathered, wh_ref[...])).astype(BF16)
             return 0
 
         lax.fori_loop(0, points // block, one, 0)
@@ -472,7 +478,7 @@
     for kx, ky in quarters:
         take(kx, ky)
     for dz in FAR(naz):
-        unpack(dz, False)
+        unpack(dz, False, dz == FAR(naz)[-1])
 
     def left(i, _):
         src = (me + i) % n
@@ -482,16 +488,6 @@
         return 0
 
     lax.fori_loop(1, n, left, 0)
-
-
-    def decode(i, _):
-        here = pl.ds(pl.multiple_of(i * block, block), block)
-        latent_out = jax.nn.gelu(total[here, :] + dot(latent[here, :].astype(BF16), ws_ref[...])).astype(BF16)
-        gathered = (cols[here, 7:8] * latent_out.astype(F32)).astype(BF16)
-        out_ref[here, :] = jax.nn.gelu(dot(gathered, wh_ref[...])).astype(BF16)
-        return 0
-
-    lax.fori_loop(0, points // block, decode, 0)
 
 
     for to_x in range(nbx):

time: 101 us -> 98 us (0.970); the launches traced: 101 us -> 97 us
  Pallas kernels: 99.7 us -> 95.6 us
    pallas_call x1, Pallas kernels: 99.7 us -> 95.6 us  [per_device(): pl.pallas_call(functools.partial(layer_kernel, (na, nb, cap, modes_y, sha...]
where the time goes in v4:
time: 98 us; the launch traced here: 97 us
  Pallas kernels  95.6 us (98%)
  matrix products  1.4 us (1%)
    pallas_call x1, Pallas kernels, per_device(): pl.pallas_call(functools.partial(layer_kernel, (na, nb, cap, modes_y, sha...  95.6 us

profile of v4, /device:TPU:0, one launch (start us, length us, event | category | flops | bytes accessed | tf_op | source)
XLA Modules:
  0.0 97.0 jit_solution(1368080250127079886)
XLA Ops:
  0.0 0.0 copy-start
  0.0 95.6 %layer.1 = bf16[2048,256]{1,0:T(8,128)(2,1)S(1)} custom-call(s32[1,2048]{1,0:T(1,128)} %bitcast.8, s32[1,2048]{1,0:T(1,128)} %bitcast.9, f32[1,2048]{1,0:T(1,128)} %bitcast.10, f32[1,2048]{1,0:T(1,128)} %bitcast.11, bf16[2048,256]{1,0:T(8,128)(2,1)} %feat_hbm.1, bf16[256,256]{1,0:T(8,128)(2,1)} %wm_hbm.1, bf16[256,256]{1,0:T(8,128)(2,1)} %ws_hbm.1, ...), custom_call_target="tpu_custom_call" | custom-call | tf_op jit(solution)/shard_map/layer/pallas_call | solution.py:545
  95.6 0.0 copy-done
  95.6 1.4 %convolution_convert_fusion = bf16[2048,256]{1,0:T(8,128)(2,1)} fusion(bf16[2048,256]{1,0:T(8,128)(2,1)S(1)} %layer.1, bf16[256,256]{1,0:T(8,128)(2,1)S(1)} %copy-done), kind=kOutput, calls=%fused_computation | convolution fusion | flops 268959744 | bytes 2228224 | tf_op jit(solution)/shard_map/dot_general | solution.py:41
Async XLA Ops:
  0.0 95.6 %copy-start = (bf16[256,256]{1,0:T(8,128)(2,1)S(1)}, bf16[256,256]{1,0:T(8,128)(2,1)}, u32[]{:S(2)}) copy-start(bf16[256,256]{1,0:T(8,128)(2,1)} %param.25) | copy-start | bytes 393220
